TPU v7x, 128 devices: a whole 4x4x4 slice. The times are simulated.
128 devices in a mesh: dp: 64 (over z, y, x), tp: 2 (over core).
Axes of the slice: x: 4, y: 4, z: 4, core: 2. Of those that a mesh axis runs over, the one named last changes fastest.
Arguments:
- hidden: bfloat16 [64, 1024, 576], P('dp')
- norm_w: bfloat16 [576], replicated
- embed_table: bfloat16 [49152, 576], P('tp')
- labels: int32 [64, 1024], P('dp')
- loss_mask: int32 [64, 1024], P('dp')
Outputs:
- output 1: float32 [], replicated
- output 2: bfloat16 [64, 1024, 576], P('dp')
- output 3: float32 [576], replicated
- output 4: float32 [49152, 576], P('tp')
All inputs are finite; a program needn't handle non-finite values.
Results may differ from a plain program's by a relative error of at most 0.001.
Values sent between devices are 32-bit elements.
A program may use at most 1 GiB of HBM per device.

v0:
```python
import jax
import jax.numpy as jnp
from jax import lax
from jax.sharding import PartitionSpec as P

SOFT_CAP = 30.0


def norm_apply(hid_rows, gain32):
    h32 = hid_rows.astype(jnp.float32)
    inv_rms = lax.rsqrt(jnp.mean(h32 * h32, axis=-1, keepdims=True) + 1e-6)
    return h32 * inv_rms * (1.0 + gain32)


def solution(mesh):
    def local_step(hidden, norm_w, embed_table, labels, loss_mask):
        batch_rows, seq_len, model_dim = hidden.shape
        vocab_local = embed_table.shape[0]
        tokens = batch_rows * seq_len
        hid_rows = hidden.reshape(tokens, model_dim)
        mask_rows = loss_mask.reshape(tokens).astype(jnp.float32)
        tok_count = jnp.maximum(lax.psum(jnp.sum(mask_rows), 'dp'), 1.0)
        normed, norm_back = jax.vjp(norm_apply, hid_rows, norm_w.astype(jnp.float32))
        normed_bf = normed.astype(jnp.bfloat16)
        logits = jnp.einsum('td,vd->tv', normed_bf, embed_table, preferred_element_type=jnp.float32)
        capped = SOFT_CAP * jnp.tanh(logits / SOFT_CAP)
        row_max = lax.pmax(jnp.max(capped, axis=-1), 'tp')
        exp_shift = jnp.exp(capped - row_max[:, None])
        row_sum = lax.psum(jnp.sum(exp_shift, axis=-1), 'tp')
        local_ids = labels.reshape(tokens) - lax.axis_index('tp') * vocab_local
        onehot = lax.broadcasted_iota(jnp.int32, (1, vocab_local), 1) == local_ids[:, None]
        picked = lax.psum(jnp.sum(jnp.where(onehot, capped, 0.0), axis=-1), 'tp')
        tok_loss = jnp.log(row_sum) + row_max - picked
        mean_loss = lax.psum(jnp.sum(mask_rows * tok_loss), 'dp') / tok_count
        tok_scale = mask_rows / tok_count
        cap_ratio = capped / SOFT_CAP
        grad_logit = ((exp_shift / row_sum[:, None] - onehot.astype(jnp.float32)) * tok_scale[:, None] * (1.0 - cap_ratio * cap_ratio)).astype(jnp.bfloat16)
        grad_part = jnp.einsum('tv,vd->td', grad_logit, embed_table, preferred_element_type=jnp.float32)
        grad_x = lax.psum(grad_part, 'tp')
        grad_rows, grad_gain = norm_back(grad_x)
        grad_gain = lax.psum(grad_gain, 'dp')
        table_part = jnp.einsum('tv,td->vd', grad_logit, normed_bf, preferred_element_type=jnp.float32)
        grad_table = lax.psum(table_part, 'dp')
        return mean_loss, grad_rows.reshape(batch_rows, seq_len, model_dim), grad_gain, grad_table

    return jax.shard_map(local_step, mesh=mesh, in_specs=(P('dp', None, None), P(None), P('tp', None), P('dp', None), P('dp', None)), out_specs=(P(), P('dp', None, None), P(None), P('tp', None)), check_vma=False)
```

profile of v0, /device:TPU:0, one launch (start us, length us, event | category | flops | bytes accessed | tf_op | source)
XLA Modules:
  0.0 975.0 jit_solution(10454260304818334009)
XLA Ops:
  7.2 0.0 all-reduce.5.cloned.1.call-start
  7.2 1.3 convert_reduce_fusion
  8.5 0.7 convert_element_type.31
  9.2 181.2 %psum.52 = f32[]{:T(128)} all-reduce(f32[]{:T(128)} %convert_reduce_fusion), channel_id=1, replica_groups=mesh['dp'=64,'tp'=2] {'dp'}, use_global_device_ids=true, to_apply=%region_10.11 | all-reduce | flops 1 | bytes 8 | tf_op jit(solution)/shard_map/psum | solution.py:22
  190.4 0.7 convert_add_fusion
  191.0 0.0 copy-start.1
  191.0 1.5 fusion.8
  192.6 0.0 copy-start.5
  192.6 0.6 copy-done.5
  193.2 0.0 copy-done.1
  193.2 0.0 copy-start.3
  193.2 0.6 copy-done.3
  193.8 1.6 fusion.14.clone.4
  195.4 0.0 copy-start.7
  195.4 57.4 %fusion.2 = (f32[1024]{0:T(1024)S(1)}, f32[1024,24576]{1,0:T(8,128)}) fusion(bf16[24576,576]{0,1:T(8,128)(2,1)} %param.7, bf16[1024,576]{0,1:T(8,128)(2,1)S(1)} %fusion.14.clone.4), kind=kOutput, calls=%fused_computation.7 | convolution fusion | flops 29066526720 | bytes 130158592 | tf_op jit(solution)/shard_map/td,vd->tv/dot_general | solution.py:25
  252.8 2.4 pmax.7
  255.9 0.0 copy-done.7
  255.9 45.2 %fusion.1 = (f32[1024]{0:T(1024)S(1)}, f32[1024]{0:T(1024)S(1)}) fusion(f32[1024,24576]{1,0:T(8,128)} %get-tuple-element.15, f32[1024]{0:T(1024)S(1)} %pmax.7, s32[1024]{0:T(1024)S(1)} %bitcast.24), kind=kLoop, calls=%fused_computation.6 | loop fusion | flops 176158720 | bytes 100679680 | tf_op jit(solution)/shard_map/reduce_sum | solution.py:29
  301.1 2.5 all-reduce.1
  303.6 0.6 broadcast_divide_fusion
  304.2 58.6 %multiply_convert_fusion = bf16[1024,24576]{1,0:T(8,128)(2,1)} fusion(f32[1024,24576]{1,0:T(8,128)} %get-tuple-element.15, f32[1024]{0:T(1024)S(1)} %get-tuple-element.12, f32[1024]{0:T(1024)S(1)} %get-tuple-element.11, s32[1024]{0:T(1024)S(1)} %bitcast.25, f32[1024]{0:T(1024)S(1)} %pmax.7), kind=kLoop, calls=%fused_computation | loop fusion | flops 301989888 | bytes 151011328 | tf_op jit(solution)/shard_map/convert_element_type | solution.py:37
  362.8 0.0 copy-start
  362.8 0.0 copy-start.2
  362.8 0.0 copy-start.4
  362.8 38.5 %fusion.16 = f32[1024,576]{0,1:T(8,128)} fusion(bf16[1024,24576]{1,0:T(8,128)(2,1)} %multiply_convert_fusion, bf16[24576,576]{0,1:T(8,128)(2,1)} %param.7), kind=kOutput, calls=%fused_computation.31 | convolution fusion | flops 28991029248 | bytes 81002496 | tf_op jit(solution)/shard_map/tv,vd->td/dot_general | solution.py:38
  401.3 0.0 all-reduce.5.cloned.1.call-update
  401.3 0.3 all-reduce.7.cloned.1.call-start
  401.6 0.0 copy-done
  401.6 0.0 copy-done.2
  401.6 0.0 copy-done.4
  401.6 45.1 %fusion.11 = f32[24576,576]{0,1:T(8,128)} fusion(bf16[1024,24576]{1,0:T(8,128)(2,1)} %multiply_convert_fusion, bf16[1,1024,576]{1,2,0:T(8,128)(2,1)S(1)} %copy-done, f32[576]{0:T(1024)S(1)} %copy-done.2, f32[1024]{0:T(1024)S(1)} %copy-done.4), kind=kOutput, calls=%fused_computation.21 | convolution fusion | flops 28993388544 | bytes 108140800 | tf_op jit(solution)/shard_map/tv,td->vd/dot_general | solution.py:42
  446.7 0.0 copy-start.6
  446.7 0.0 all-reduce.7.cloned.1.call-update
  446.7 0.0 all-reduce.5.cloned.1.call-done
  446.7 2.5 fusion.6
  449.2 179.5 %all-reduce = (f32[]{:T(128)}, f32[576]{0:T(1024)}) all-reduce(f32[]{:T(128)} %get-tuple-element.13, f32[576]{0:T(1024)S(1)} %get-tuple-element.6), channel_id=1, replica_groups=mesh['dp'=64,'tp'=2] {'dp'}, use_global_device_ids=true, to_apply=%region_8.9 | all-reduce | flops 577 | bytes 4616 | tf_op jit(solution)/shard_map/psum | solution.py:34
  629.4 0.0 copy-done.6
  629.4 3.2 fusion.10
  632.6 295.9 %all-reduce.7.cloned.1.call-done = f32[24576,576]{0,1:T(8,128)} async-done(((f32[24576,576]{0,1:T(8,128)}), f32[24576,576]{0,1:T(8,128)}) %all-reduce.7.cloned.1.call-update) | async-done | bytes 56623120 | tf_op jit(solution)/shard_map/psum | solution.py:43
  928.5 38.6 %copy.11 = f32[24576,576]{0,1:T(8,128)} copy(f32[24576,576]{0,1:T(8,128)} %all-reduce.7.cloned.1.call-done) | data formatting | bytes 113246208
  (3 shorter events, 0.0 us)
Async XLA Ops:
  7.2 439.5 %all-reduce.5.cloned.1.call-start = ((), (), s32[]{:S(2)}) async-start(), calls=%async_computation | async-start | bytes 4718592 | tf_op jit(solution)/shard_map/psum | solution.py:39
  191.0 2.1 copy-start.1
  192.6 0.6 copy-start.5
  193.2 0.6 copy-start.3
  195.4 60.5 %copy-start.7 = (s32[1,1024]{1,0:T(1,128)S(1)}, s32[1,1024]{1,0:T(1,128)}, u32[]{:S(2)}) copy-start(s32[1,1024]{1,0:T(1,128)} %param.8) | copy-start | bytes 12292
  362.8 38.8 %copy-start = (bf16[1,1024,576]{1,2,0:T(8,128)(2,1)S(1)}, bf16[1,1024,576]{1,2,0:T(8,128)(2,1)}, u32[]{:S(2)}) copy-start(bf16[1,1024,576]{1,2,0:T(8,128)(2,1)} %param.5) | copy-start | bytes 3538948
  362.8 38.8 %copy-start.2 = (f32[576]{0:T(1024)S(1)}, f32[576]{0:T(1024)}, u32[]{:S(2)}) copy-start(f32[576]{0:T(1024)} %copy-done.1) | copy-start | bytes 6916
  362.8 38.8 %copy-start.4 = (f32[1024]{0:T(1024)S(1)}, f32[1024]{0:T(1024)}, u32[]{:S(2)}) copy-start(f32[1024]{0:T(1024)} %copy-done.3) | copy-start | bytes 12292
  401.3 527.2 %all-reduce.7.cloned.1.call-start = ((), (), s32[]{:S(2)}) async-start(), calls=%async_computation.1 | async-start | bytes 113246208 | tf_op jit(solution)/shard_map/psum | solution.py:43
  446.7 182.7 %copy-start.6 = (f32[1024]{0:T(1024)S(1)}, f32[1024]{0:T(1024)}, u32[]{:S(2)}) copy-start(f32[1024]{0:T(1024)} %copy-done.5) | copy-start | bytes 12292
Sparse Core Ops, SparseCore 0:
  401.4 19.8 all-reduce.4
  446.8 481.6 all-reduce.6
where the time goes:
time: 975 us
  blocking collectives  366 us (38%)
  waiting for transfers between devices  296 us (30%)
  matrix products  141 us (14%)
  other arithmetic  116 us (12%)
  local copies, waits for them, and re-layouts  39.8 us (4%)
  between operations  16.6 us (2%)
    psum x1, waiting for transfers between devices, local_step(): grad_table = lax.psum(table_part, 'dp')  296 us
    psum x1, blocking collectives, local_step(): tok_count = jnp.maximum(lax.psum(jnp.sum(mask_rows), 'dp'), 1.0)  181 us
    psum x1, blocking collectives, local_step(): mean_loss = lax.psum(jnp.sum(mask_rows * tok_loss), 'dp') / tok_count  180 us
    convert_element_type x1, other arithmetic, local_step(): ((exp_shift / row_sum[:, None] - onehot.astype(jnp.float32)) * tok_scale[...  58.6 us
    dot_general x1, matrix products, local_step(): jnp.einsum('td,vd->tv', normed_bf, embed_table, preferred_element_type=jn...  57.4 us
    reduce_sum x1, other arithmetic, local_step(): row_sum = lax.psum(jnp.sum(exp_shift, axis=-1), 'tp')  45.2 us
    dot_general x1, matrix products, local_step(): jnp.einsum('tv,td->vd', grad_logit, normed_bf, preferred_element_type=jnp...  45.1 us
    unnamed x17, local copies, waits for them, and re-layouts  39.8 us
  transfers between devices with their start and end apart: 2, of which 1 were waited for; matrix products, arithmetic and copies ran while one was open for 5% of the time, Pallas kernels for 0%

commit v1 on v0

v1 whole, which is shorter than its diff:
```python
import jax
import jax.numpy as jnp
import numpy as np
from jax import lax
from jax.experimental import pallas as pl
from jax.experimental.pallas import tpu as pltpu
from jax.sharding import Mesh, PartitionSpec as P

SOFT_CAP = 30.0
INV_CAP = 1.0 / SOFT_CAP
CAP_LOG2E = SOFT_CAP * 1.4426950408889634
LANES = 128
NCHUNK = 3
VMEM_LIMIT = 60 * 1024 * 1024
F32 = jnp.float32
BF16 = jnp.bfloat16
FAR = -(2 ** 24)


def norm_body(ht_ref, w1_ref, xt_ref, xb_ref):
    h = ht_ref[...].astype(F32)
    inv_rms = lax.rsqrt(jnp.mean(h * h, axis=0, keepdims=True) + 1e-6)
    xt = h * inv_rms * jnp.broadcast_to(w1_ref[:, :1], h.shape)
    xt_ref[...] = xt
    xb_ref[...] = xt.T.astype(BF16)


def norm_rows(ht, w1):
    dim, tokens = ht.shape
    tb = min(512, tokens)
    return pl.pallas_call(
        norm_body,
        grid=(tokens // tb,),
        in_specs=[
            pl.BlockSpec((dim, tb), lambda i: (0, i)),
            pl.BlockSpec((dim, LANES), lambda i: (0, 0)),
        ],
        out_specs=[
            pl.BlockSpec((dim, tb), lambda i: (0, i)),
            pl.BlockSpec((tb, dim), lambda i: (i, 0)),
        ],
        out_shape=[
            jax.ShapeDtypeStruct((dim, tokens), F32),
            jax.ShapeDtypeStruct((tokens, dim), BF16),
        ],
        compiler_params=pltpu.CompilerParams(
            dimension_semantics=("arbitrary",), vmem_limit_bytes=VMEM_LIMIT),
        cost_estimate=pl.CostEstimate(
            flops=10 * dim * tokens, bytes_accessed=8 * dim * tokens, transcendentals=0),
        name="norm",
    )(ht, w1)


def norm_back_body(ht_ref, w1_ref, g0_ref, g1_ref, dh_ref, dw_ref):
    h = ht_ref[...].astype(F32)
    inv_rms = lax.rsqrt(jnp.mean(h * h, axis=0, keepdims=True) + 1e-6)
    n = h * inv_rms
    g = g0_ref[...] + g1_ref[...]
    gn = g * n

    @pl.when(pl.program_id(0) == 0)
    def _():
        dw_ref[...] = jnp.zeros_like(dw_ref)

    part = dw_ref[...]
    for j in range(h.shape[1] // LANES):
        part = part + gn[:, j * LANES:(j + 1) * LANES]
    dw_ref[...] = part
    w1 = jnp.broadcast_to(w1_ref[:, :1], h.shape)
    inner = jnp.mean(gn * w1, axis=0, keepdims=True)
    dh_ref[...] = ((g * w1 - n * inner) * inv_rms).astype(BF16)


def norm_back(ht, w1, g0, g1):
    dim, tokens = ht.shape
    tb = min(512, tokens)
    return pl.pallas_call(
        norm_back_body,
        grid=(tokens // tb,),
        in_specs=[
            pl.BlockSpec((dim, tb), lambda i: (0, i)),
            pl.BlockSpec((dim, LANES), lambda i: (0, 0)),
            pl.BlockSpec((dim, tb), lambda i: (0, i)),
            pl.BlockSpec((dim, tb), lambda i: (0, i)),
        ],
        out_specs=[
            pl.BlockSpec((dim, tb), lambda i: (0, i)),
            pl.BlockSpec((dim, LANES), lambda i: (0, 0)),
        ],
        out_shape=[
            jax.ShapeDtypeStruct((dim, tokens), BF16),
            jax.ShapeDtypeStruct((dim, LANES), F32),
        ],
        compiler_params=pltpu.CompilerParams(
            dimension_semantics=("arbitrary",), vmem_limit_bytes=VMEM_LIMIT),
        cost_estimate=pl.CostEstimate(
            flops=20 * dim * tokens, bytes_accessed=12 * dim * tokens, transcendentals=0),
        name="norm_back",
    )(ht, w1, g0, g1)


def dot_f32(a, b, dims):
    return lax.dot_general(a, b, (dims, ((), ())), preferred_element_type=F32)


def fwd_body(tb, x_ref, lab_ref, e_ref, z_ref, p_ref):
    step = pl.program_id(0)
    tokens = x_ref.shape[0]
    bv = e_ref.shape[1]

    @pl.when(step == 0)
    def _():
        z_ref[...] = jnp.zeros_like(z_ref)
        p_ref[...] = jnp.zeros_like(p_ref)

    lane = lax.broadcasted_iota(jnp.int32, (tb, LANES), 1)

    def block(i, carry):
        rows = pl.ds(pl.multiple_of(i * tb, tb), tb)
        z = dot_f32(x_ref[rows, :], e_ref[...], ((1,), (0,)))
        lab = lab_ref[rows, :] - step * bv
        zsum = z_ref[rows, :]
        psum = p_ref[rows, :]
        for j in range(bv // LANES):
            t = jnp.tanh(z[:, j * LANES:(j + 1) * LANES] * INV_CAP)
            zsum = zsum + jnp.exp2(t * CAP_LOG2E)
            psum = jnp.where(lab == lane + j * LANES, t, psum)
        z_ref[rows, :] = zsum
        p_ref[rows, :] = psum
        return carry

    lax.fori_loop(0, tokens // tb, block, 0, unroll=True)


def forward(x, lab_rep, et, bv=512, tb=256):
    tokens, dim = x.shape
    vocab = et.shape[1]
    tb = min(tb, tokens)
    return pl.pallas_call(
        lambda *refs: fwd_body(tb, *refs),
        grid=(vocab // bv,),
        in_specs=[
            pl.BlockSpec((tokens, dim), lambda i: (0, 0)),
            pl.BlockSpec((tokens, LANES), lambda i: (0, 0)),
            pl.BlockSpec((dim, bv), lambda i: (0, i)),
        ],
        out_specs=[
            pl.BlockSpec((tokens, LANES), lambda i: (0, 0)),
            pl.BlockSpec((tokens, LANES), lambda i: (0, 0)),
        ],
        out_shape=[jax.ShapeDtypeStruct((tokens, LANES), F32)] * 2,
        compiler_params=pltpu.CompilerParams(
            dimension_semantics=("arbitrary",), vmem_limit_bytes=VMEM_LIMIT),
        cost_estimate=pl.CostEstimate(
            flops=2 * tokens * dim * vocab, bytes_accessed=2 * dim * vocab,
            transcendentals=2 * tokens * vocab),
        name="fwd",
    )(x, lab_rep, et)


def prep_body(xt_ref, xtb_ref, xb_ref):
    xt = xt_ref[0]
    xtb_ref[...] = xt.astype(BF16)
    xb_ref[...] = xt.T.astype(BF16)


def prep(xgt):
    group, dim, tokens = xgt.shape
    return pl.pallas_call(
        prep_body,
        grid=(group,),
        in_specs=[pl.BlockSpec((1, dim, tokens), lambda i: (i, 0, 0))],
        out_specs=[
            pl.BlockSpec((dim, tokens), lambda i: (0, i)),
            pl.BlockSpec((tokens, dim), lambda i: (i, 0)),
        ],
        out_shape=[
            jax.ShapeDtypeStruct((dim, group * tokens), BF16),
            jax.ShapeDtypeStruct((group * tokens, dim), BF16),
        ],
        compiler_params=pltpu.CompilerParams(
            dimension_semantics=("arbitrary",), vmem_limit_bytes=VMEM_LIMIT),
        cost_estimate=pl.CostEstimate(
            flops=10 * group * dim * tokens, bytes_accessed=8 * group * dim * tokens,
            transcendentals=0),
        name="prep",
    )(xgt)


def grad_tile(z, scale, lab, vid, inv_count):
    t = jnp.tanh(z * INV_CAP)
    p = jnp.exp2(t * CAP_LOG2E) * scale
    p = jnp.where(lab == vid, p - inv_count, p)
    return (p * (1.0 - t * t)).astype(BF16)


def table_body(chunk, stride, tb, idx_ref, cnt_ref, xb_ref, xtb_ref, scale_ref, lab_ref,
               e0_ref, e1_ref, out_ref, ga_ref, gb_ref, et_ref, acc_ref):
    step = pl.program_id(0)
    blocks = xb_ref.shape[0] // tb
    inv_count = cnt_ref[0]
    et_ref[:, :LANES] = e0_ref[...]
    et_ref[:, LANES:] = e1_ref[...]
    lane = lax.broadcasted_iota(jnp.int32, (tb, LANES), 1)
    base = chunk + step * 2 * stride

    def rows_of(i):
        return pl.ds(pl.multiple_of(i * tb, tb), tb)

    def grads(i, g_ref):
        rows = rows_of(i)
        z = dot_f32(xb_ref[rows, :], et_ref[...], ((1,), (0,)))
        lab = lab_ref[rows, :] - base
        scale = scale_ref[rows, :]
        for j in range(2):
            g_ref[:, j * LANES:(j + 1) * LANES] = grad_tile(
                z[:, j * LANES:(j + 1) * LANES], scale, lab, lane + j * stride, inv_count)

    def product(i, g_ref):
        return dot_f32(xtb_ref[:, rows_of(i)], g_ref[...], ((1,), (0,)))

    grads(0, ga_ref)
    grads(1, gb_ref)
    acc_ref[...] = product(0, ga_ref)

    def pair(k, carry):
        grads(2 * k, ga_ref)
        acc_ref[...] += product(2 * k - 1, gb_ref)
        grads(2 * k + 1, gb_ref)
        acc_ref[...] += product(2 * k, ga_ref)
        return carry

    lax.fori_loop(1, blocks // 2, pair, 0)
    last = product(blocks - 1, gb_ref)
    out_ref[0] = acc_ref[:, :LANES] + last[:, :LANES]
    out_ref[1] = acc_ref[:, LANES:] + last[:, LANES:]


def table_chunk(c, idx, inv_count, xb, xtb, scale_rep, lab_rep, et, n_dest, group, tb=512):
    tokens, dim = xb.shape
    tb = min(tb, tokens // 2)
    first = c * n_dest * group

    def whole(shape):
        return pl.BlockSpec(shape, lambda i, idx: (0, 0), pipeline_mode=pl.Buffered(1))

    def e_spec(k):
        return pl.BlockSpec((dim, LANES), lambda i, idx: (0, first + (2 * i + k) * group + idx[0]))

    return pl.pallas_call(
        lambda *refs: table_body(first * LANES, group * LANES, tb, *refs),
        grid_spec=pltpu.PrefetchScalarGridSpec(
            num_scalar_prefetch=1,
            grid=(n_dest // 2,),
            in_specs=[
                pl.BlockSpec(memory_space=pltpu.SMEM),
                whole((tokens, dim)),
                whole((dim, tokens)),
                whole((tokens, LANES)),
                whole((tokens, LANES)),
                e_spec(0),
                e_spec(1),
            ],
            out_specs=[pl.BlockSpec((2, dim, LANES), lambda i, idx: (i, 0, 0))],
            scratch_shapes=[
                pltpu.VMEM((tb, 2 * LANES), BF16),
                pltpu.VMEM((tb, 2 * LANES), BF16),
                pltpu.VMEM((dim, 2 * LANES), BF16),
                pltpu.VMEM((dim, 2 * LANES), F32),
            ],
        ),
        out_shape=[jax.ShapeDtypeStruct((n_dest, dim, LANES), F32)],
        compiler_params=pltpu.CompilerParams(
            dimension_semantics=("arbitrary",), vmem_limit_bytes=VMEM_LIMIT),
        cost_estimate=pl.CostEstimate(
            flops=4 * tokens * dim * n_dest * LANES,
            bytes_accessed=6 * dim * n_dest * LANES + 4 * tokens * dim,
            transcendentals=2 * tokens * n_dest * LANES),
        name="table_grad",
    )(idx, inv_count, xb, xtb, scale_rep, lab_rep, et, et)[0]


def rows_body(tb, cnt_ref, x_ref, scale_ref, lab_ref, e_ref, out_ref, g_ref):
    step = pl.program_id(0)
    tokens = x_ref.shape[0]
    bv = e_ref.shape[1]
    inv_count = cnt_ref[0]

    @pl.when(step == 0)
    def _():
        out_ref[...] = jnp.zeros_like(out_ref)

    lane = lax.broadcasted_iota(jnp.int32, (tb, LANES), 1)

    def block(i, carry):
        rows = pl.ds(pl.multiple_of(i * tb, tb), tb)
        z = dot_f32(x_ref[rows, :], e_ref[...], ((1,), (0,)))
        lab = lab_ref[rows, :] - step * bv
        scale = scale_ref[rows, :]
        for j in range(bv // LANES):
            g_ref[:, j * LANES:(j + 1) * LANES] = grad_tile(
                z[:, j * LANES:(j + 1) * LANES], scale, lab, lane + j * LANES, inv_count)
        out_ref[:, rows] += dot_f32(e_ref[...], g_ref[...], ((1,), (1,)))
        return carry

    lax.fori_loop(0, tokens // tb, block, 0)


def rows_grad(inv_count, x, scale_rep, lab_rep, et, bv=1024, tb=256):
    tokens, dim = x.shape
    vocab = et.shape[1]
    tb = min(tb, tokens)
    return pl.pallas_call(
        lambda *refs: rows_body(tb, *refs),
        grid=(vocab // bv,),
        in_specs=[
            pl.BlockSpec(memory_space=pltpu.SMEM),
            pl.BlockSpec((tokens, dim), lambda i: (0, 0)),
            pl.BlockSpec((tokens, LANES), lambda i: (0, 0)),
            pl.BlockSpec((tokens, LANES), lambda i: (0, 0)),
            pl.BlockSpec((dim, bv), lambda i: (0, i)),
        ],
        out_specs=[pl.BlockSpec((dim, tokens), lambda i: (0, 0))],
        out_shape=[jax.ShapeDtypeStruct((dim, tokens), F32)],
        scratch_shapes=[pltpu.VMEM((tb, bv), BF16)],
        compiler_params=pltpu.CompilerParams(
            dimension_semantics=("arbitrary",), vmem_limit_bytes=VMEM_LIMIT),
        cost_estimate=pl.CostEstimate(
            flops=4 * tokens * dim * vocab, bytes_accessed=2 * dim * vocab,
            transcendentals=2 * tokens * vocab),
        name="rows_grad",
    )(inv_count, x, scale_rep, lab_rep, et)[0]


def place_body(n, src_ref, *refs):
    out_ref = refs[-1]
    for k in range(n):
        out_ref[:, k * LANES:(k + 1) * LANES] = src_ref[k]


def place_chunk(c, gathered, table, vocab):
    n_dev, dim, _ = gathered.shape
    rows = 96 if dim % 96 == 0 else dim
    out_shape = jax.ShapeDtypeStruct((dim, vocab), F32)
    in_specs = [pl.BlockSpec((n_dev, rows, LANES), lambda i: (0, i, 0))]
    args = [gathered]
    alias = {}
    if table is not None:
        in_specs.append(pl.BlockSpec(memory_space=pl.ANY))
        args.append(table)
        alias = {1: 0}
    return pl.pallas_call(
        lambda *refs: place_body(n_dev, *refs),
        grid=(dim // rows,),
        in_specs=in_specs,
        out_specs=pl.BlockSpec((rows, n_dev * LANES), lambda i: (i, c)),
        out_shape=out_shape,
        input_output_aliases=alias,
        compiler_params=pltpu.CompilerParams(
            dimension_semantics=("arbitrary",), vmem_limit_bytes=VMEM_LIMIT),
        cost_estimate=pl.CostEstimate(
            flops=n_dev * dim * LANES, bytes_accessed=8 * n_dev * dim * LANES, transcendentals=0),
        name="place",
    )(*args)


def solution(mesh, dims=(4, 4, 4)):
    nz, ny, nx = dims
    grid_mesh = Mesh(mesh.devices.reshape(nz, ny, nx, 2), ('z', 'y', 'x', 'core'))
    every = ('z', 'y', 'x', 'core')

    def local_step(hidden, norm_w, embed_table, labels, loss_mask):
        batch_rows, seq_len, dim = hidden.shape
        vocab = embed_table.shape[0]
        tokens = batch_rows * seq_len
        n_dest = nz * ny
        et = embed_table.T
        ht = hidden.reshape(tokens, dim).T
        w1 = jnp.broadcast_to((1.0 + norm_w.astype(F32))[:, None], (dim, LANES))
        mask_rows = loss_mask.reshape(tokens).astype(F32)
        core = lax.axis_index('core')
        x_idx = lax.axis_index('x')

        count = jnp.maximum(lax.psum(jnp.sum(mask_rows), every) * 0.5, 1.0)
        xt_own, xb_own = norm_rows(ht, w1)
        xgt = lax.all_gather(xt_own, 'x', axis=0)

        lab_own = labels.reshape(tokens)
        lab_local = lab_own - core * vocab
        zpart, ppart = forward(
            xb_own, jnp.broadcast_to(lab_local[:, None], (tokens, LANES)), et)

        lab_masked = jnp.where(mask_rows > 0.0, lab_own, FAR).astype(F32)
        stats = lax.all_gather(
            jnp.stack([jnp.sum(zpart, axis=1), jnp.sum(ppart, axis=1), lab_masked]),
            ('x', 'core'), axis=0).reshape(nx, 2, 3, tokens)
        row_sum = stats[:, 0, 0] + stats[:, 1, 0]
        lab_group = stats[:, 0, 2].astype(jnp.int32)
        picked = lax.dynamic_index_in_dim(stats[:, 0, 1] + stats[:, 1, 1], x_idx, 0, False) * SOFT_CAP
        own_sum = lax.dynamic_index_in_dim(row_sum, x_idx, 0, False)
        tok_loss = jnp.log(own_sum) - picked
        loss_part = jnp.sum(mask_rows * tok_loss)

        inv_count = 1.0 / count
        scale_group = jnp.where(lab_group >= 0, inv_count, 0.0) / row_sum
        scale_own = (mask_rows * inv_count) / own_sum
        cnt = inv_count.reshape(1)
        group_tokens = nx * tokens
        scale_rep = jnp.broadcast_to(scale_group.reshape(group_tokens, 1), (group_tokens, LANES))
        lab_rep = jnp.broadcast_to(
            (lab_group - core * vocab - x_idx * LANES).reshape(group_tokens, 1), (group_tokens, LANES))

        xtb, xb = prep(xgt)
        idx = x_idx.astype(jnp.int32).reshape(1)
        table = None
        for c in range(NCHUNK):
            part = table_chunk(c, idx, cnt, xb, xtb, scale_rep, lab_rep, et, n_dest, nx)
            mine = lax.psum_scatter(part, ('z', 'y'), scatter_dimension=0, tiled=False)
            gathered = lax.all_gather(mine, ('z', 'y', 'x'), axis=0)
            table = place_chunk(c, gathered, table, vocab)

        xb_late, _ = lax.optimization_barrier((xb_own, part))
        lab_mine = jnp.where(mask_rows > 0.0, lab_local, FAR)
        gxt = rows_grad(
            cnt, xb_late, jnp.broadcast_to(scale_own[:, None], (tokens, LANES)),
            jnp.broadcast_to(lab_mine[:, None], (tokens, LANES)), et)
        dht, dw = norm_back(ht, w1, gxt, lax.ppermute(gxt, 'core', [(0, 1), (1, 0)]))
        grad_rows = dht.T
        loss_sum, grad_gain = lax.psum((loss_part, jnp.sum(dw, axis=1)), every)
        return (loss_sum * 0.5 / count, grad_rows.reshape(batch_rows, seq_len, dim),
                grad_gain * 0.5, table.T)

    dp = ('z', 'y', 'x')
    return jax.shard_map(
        local_step, mesh=grid_mesh,
        in_specs=(P(dp, None, None), P(None), P('core', None), P(dp, None), P(dp, None)),
        out_specs=(P(), P(dp, None, None), P(None), P('core', None)), check_vma=False)
```

time: 975 us -> 820 us (0.84)
  Pallas kernels: 0 us -> 389 us
  blocking collectives: 366 us -> 150 us
  matrix products: 141 us -> 0 us
  other arithmetic: 116 us -> 7.68 us
  waiting for transfers between devices: 296 us -> 244 us
  local copies, waits for them, and re-layouts: 39.8 us -> 10.1 us
    pallas_call x0 -> x11, Pallas kernels: none -> 389 us  [the longest x3 149 us: table_chunk(): pl.pallas_call(lambda *refs: table_body(first * LANES, group * LANES, tb,...]
    psum x2 -> x0, waiting for transfers between devices: 296 us -> none  [the longest x1 296 us: local_step(): grad_table = lax.psum(table_part, 'dp')]
    psum x3 -> x2, blocking collectives: 363 us -> 137 us  [the longest x1 70.1 us: local_step(): count = jnp.maximum(lax.psum(jnp.sum(mask_rows), every) * 0.5, 1.0)]
    dot_general x3 -> x0, matrix products: 141 us -> none  [the longest x1 57.4 us: local_step(): jnp.einsum('td,vd->tv', normed_bf, embed_table, preferred_element_type=jn...]
    unnamed x2 -> x10, waiting for transfers between devices: 0.03 us -> 140 us
    all_gather x0 -> x4, waiting for transfers between devices: none -> 99.7 us  [the longest x3 99.6 us: local_step(): gathered = lax.all_gather(mine, ('z', 'y', 'x'), axis=0)]
    convert_element_type x2 -> x0, other arithmetic: 59.2 us -> none  [the longest x1 58.6 us: local_step(): ((exp_shift / row_sum[:, None] - onehot.astype(jnp.float32)) * tok_scale[...]
    reduce_sum x4, other arithmetic: 50.5 us -> 4.94 us  [the longest x1 1.3 us: local_step(): count = jnp.maximum(lax.psum(jnp.sum(mask_rows), every) * 0.5, 1.0)]
  transfers between devices with their start and end apart: 2 -> 8, of which waited for: 1 -> 5; matrix products, arithmetic and copies ran while one was open for 5% -> 1% of each run, Pallas kernels for 0% -> 38%
where the time goes in v1:
time: 820 us; the launch traced here: 818 us
  Pallas kernels  389 us (47%)
  waiting for transfers between devices  244 us (30%)
  blocking collectives  150 us (18%)
  between operations  16.7 us (2%)
  local copies, waits for them, and re-layouts  10.1 us (1%)
    pallas_call x3, Pallas kernels, table_chunk(): pl.pallas_call(lambda *refs: table_body(first * LANES, group * LANES, tb,...  149 us
    unnamed x10, waiting for transfers between devices  140 us
    pallas_call x1, Pallas kernels, rows_grad(): pl.pallas_call(lambda *refs: rows_body(tb, *refs), grid=(vocab // bv,), i...  126 us
    all_gather x3, waiting for transfers between devices, local_step(): gathered = lax.all_gather(mine, ('z', 'y', 'x'), axis=0)  99.6 us
    psum x1, blocking collectives, local_step(): count = jnp.maximum(lax.psum(jnp.sum(mask_rows), every) * 0.5, 1.0)  70.1 us
    psum x1, blocking collectives, local_step(): loss_sum, grad_gain = lax.psum((loss_part, jnp.sum(dw, axis=1)), every)  67.1 us
    pallas_call x1, Pallas kernels, forward(): pl.pallas_call(lambda *refs: fwd_body(tb, *refs), grid=(vocab // bv,), in...  54.8 us
    pallas_call x3, Pallas kernels, place_chunk(): pl.pallas_call(lambda *refs: place_body(n_dev, *refs), grid=(dim // rows,...  42.2 us
  transfers between devices with their start and end apart: 8, of which 5 were waited for; matrix products, arithmetic and copies ran while one was open for 1% of the time, Pallas kernels for 38%

profile of v1, /device:TPU:0, one launch (start us, length us, event | category | flops | bytes accessed | tf_op | source)
XLA Modules:
  0.0 817.7 jit_solution(17549469844631691240)
XLA Ops:
  7.2 0.0 all-gather.14.cloned.1.call-start
  7.2 0.7 convert_add_fusion
  7.9 0.9 broadcast_in_dim.27.w1_ref
  8.8 3.3 norm.1
  12.1 0.0 all-gather.14.cloned.1.call-update
  12.1 0.0 reduce-scatter.14.cloned.1.call-start
  12.1 1.3 convert_reduce_fusion
  13.4 70.1 %psum.22 = f32[]{:T(128)} all-reduce(f32[]{:T(128)} %convert_reduce_fusion), channel_id=1, replica_groups=mesh['z'=4,'y'=4,'x'=4,'core'=2] {'z','y','x','core'}, use_global_device_ids=true, to_apply=%region_5.6 | all-reduce | flops 1 | bytes 8 | tf_op jit(solution)/shard_map/psum | solution.py:384
  83.6 0.7 broadcast_subtract_fusion
  84.3 1.0 broadcast_in_dim.50.refs_1_
  85.3 54.8 %fwd.1 = (f32[1024,128]{1,0:T(8,128)}, f32[1024,128]{1,0:T(8,128)}) custom-call(bf16[1024,576]{1,0:T(8,128)(2,1)} %get-tuple-element.19.refs_0_.refs_1_, s32[1024,128]{1,0:T(8,128)} %broadcast_in_dim.50.refs_1_, bf16[576,24576]{1,0:T(8,128)(2,1)} %bitcast.23), custom_call_target="tpu_custom_call" | custom-call | flops 28991029248 | bytes 28311552 | tf_op jit(solution)/shard_map/fwd/pallas_call | solution.py:139
  140.1 1.2 reduce_sum.45
  141.3 1.2 reduce_sum.46
  143.3 12.8 %all-gather.2 = f32[8,3,1024]{2,1,0:T(4,128)S(1)} all-gather(f32[1,3,1024]{2,1,0:T(4,128)S(1)} %maximum_bitcast_fusion), channel_id=2, replica_groups=mesh['z'=4,'y'=4,'x'=4,'core'=2] {'x','core'}, dimensions={0}, use_global_device_ids=true | all-gather | bytes 110592 | tf_op jit(solution)/shard_map/all_gather | solution.py:394
  156.1 0.1 fusion
  156.2 0.0 all-gather.14.cloned.1.call-done
  156.2 8.1 prep.1
  164.2 2.9 broadcast_in_dim.55.refs_5_
  167.1 1.9 broadcast_in_dim.54.refs_4_
  169.0 49.8 %table_grad.5 = f32[16,576,128]{2,1,0:T(8,128)} custom-call(s32[1]{0:T(128)} %bitcast.13.refs_0_, f32[1]{0:T(128)} %bitcast.12.refs_1_.refs_0_, bf16[4096,576]{1,0:T(8,128)(2,1)} %get-tuple-element.17.refs_2_, bf16[576,4096]{1,0:T(8,128)(2,1)} %get-tuple-element.18.refs_3_, f32[4096,128]{1,0:T(8,128)} %broadcast_in_dim.54.refs_4_, ...), custom_call_target="tpu_custom_call" | custom-call | flops 19327352832 | bytes 16515072 | tf_op jit(solution)/shard_map/table_grad/pallas_call | solution.py:250
  218.9 0.0 reduce-scatter.14.cloned.1.call-update
  218.9 0.0 reduce-scatter.12.cloned.1.call-start
  218.9 49.8 %table_grad.4 = f32[16,576,128]{2,1,0:T(8,128)} custom-call(s32[1]{0:T(128)} %bitcast.13.refs_0_, f32[1]{0:T(128)} %bitcast.12.refs_1_.refs_0_, bf16[4096,576]{1,0:T(8,128)(2,1)} %get-tuple-element.17.refs_2_, bf16[576,4096]{1,0:T(8,128)(2,1)} %get-tuple-element.18.refs_3_, f32[4096,128]{1,0:T(8,128)} %broadcast_in_dim.54.refs_4_, ...), custom_call_target="tpu_custom_call" | custom-call | flops 19327352832 | bytes 16515072 | tf_op jit(solution)/shard_map/table_grad/pallas_call | solution.py:250
  268.7 0.2 reduce-scatter.10.cloned.1.call-start
  269.0 49.8 %table_grad.3 = f32[16,576,128]{2,1,0:T(8,128)} custom-call(s32[1]{0:T(128)} %bitcast.13.refs_0_, f32[1]{0:T(128)} %bitcast.12.refs_1_.refs_0_, bf16[4096,576]{1,0:T(8,128)(2,1)} %get-tuple-element.17.refs_2_, bf16[576,4096]{1,0:T(8,128)(2,1)} %get-tuple-element.18.refs_3_, f32[4096,128]{1,0:T(8,128)} %broadcast_in_dim.54.refs_4_, ...), custom_call_target="tpu_custom_call" | custom-call | flops 19327352832 | bytes 16515072 | tf_op jit(solution)/shard_map/table_grad/pallas_call | solution.py:250
  318.8 0.0 reduce-scatter.10.cloned.1.call-update
  318.8 0.0 all-gather.12.cloned.1.call-start
  318.9 0.0 reduce-scatter.14.cloned.1.call-done
  318.9 0.5 all-gather.12.cloned.1.call-update
  319.4 0.0 all-gather.10.cloned.1.call-start
  319.4 57.5 %reduce-scatter.12.cloned.1.call-done = f32[1,576,128]{2,1,0:T(8,128)} async-done(((f32[16,576,128]{2,1,0:T(8,128)}), f32[1,576,128]{2,1,0:T(8,128)}) %reduce-scatter.12.cloned.1.call-update) | async-done | bytes 294928
  377.0 0.0 all-gather.8.cloned.1.call-start
  377.1 81.7 %reduce-scatter.10.cloned.1.call-done = f32[1,576,128]{2,1,0:T(8,128)} async-done(((f32[16,576,128]{2,1,0:T(8,128)}), f32[1,576,128]{2,1,0:T(8,128)}) %reduce-scatter.10.cloned.1.call-update) | async-done | bytes 294928
  458.8 0.6 multiply_divide_fusion
  459.4 1.0 broadcast_in_dim.56.refs_2_
  460.4 1.0 broadcast_in_dim.58.refs_3_
  461.4 126.0 %rows_grad.1.g0_ref = f32[576,1024]{1,0:T(8,128)} custom-call(f32[1]{0:T(128)} %bitcast.12.refs_1_.refs_0_, bf16[1024,576]{1,0:T(8,128)(2,1)} %get-tuple-element.19.refs_0_.refs_1_, f32[1024,128]{1,0:T(8,128)} %broadcast_in_dim.56.refs_2_, s32[1024,128]{1,0:T(8,128)} %broadcast_in_dim.58.refs_3_, bf16[576,24576]{1,0:T(8,128)(2,1)} %bitcast.30), custom_call_target="tpu_custom_call" | custom-call | flops 57982058496 | bytes 28311552 | tf_op jit(solution)/shard_map/rows_grad/pallas_call | solution.py:313
  587.4 4.5 collective-permute-done.g1_ref
  591.9 1.4 copy-done
  593.3 5.0 norm_back.1
  598.4 1.1 reduce_sum.49
  599.5 67.1 %all-reduce.3 = (f32[]{:T(128)}, f32[576]{0:T(1024)S(1)}) all-reduce(f32[]{:T(128)} %get-tuple-element.29, f32[576]{0:T(1024)S(1)} %reduce_sum.49), channel_id=1, replica_groups=mesh['z'=4,'y'=4,'x'=4,'core'=2] {'z','y','x','core'}, use_global_device_ids=true, to_apply=%region_3.4 | all-reduce | flops 577 | bytes 4616 | tf_op jit(solution)/shard_map/psum | solution.py:429
  667.3 0.6 broadcast_multiply_fusion
  667.9 14.1 %place.3.refs_1_ = f32[576,24576]{1,0:T(8,128)} custom-call(f32[64,576,128]{2,1,0:T(8,128)} %all-gather.12.cloned.1.call-done.refs_0_), custom_call_target="tpu_custom_call" | custom-call | flops 4718592 | bytes 37748736 | tf_op jit(solution)/shard_map/place/pallas_call | solution.py:352
  682.0 2.0 all-gather.10.cloned.1.call-done.refs_0_
  683.9 14.1 %place.4.refs_1_ = f32[576,24576]{1,0:T(8,128)} custom-call(f32[64,576,128]{2,1,0:T(8,128)} %all-gather.10.cloned.1.call-done.refs_0_, f32[576,24576]{1,0:T(8,128)} %place.3.refs_1_), custom_call_target="tpu_custom_call", output_to_operand_aliasing={{}: (1, {})} | custom-call | flops 4718592 | bytes 37748736 | tf_op jit(solution)/shard_map/place/pallas_call | solution.py:352
  698.0 97.7 %all-gather.8.cloned.1.call-done.refs_0_ = f32[64,576,128]{2,1,0:T(8,128)} async-done(((f32[1,576,128]{2,1,0:T(8,128)}), f32[64,576,128]{2,1,0:T(8,128)}) %all-gather.8.cloned.1.call-update) | async-done | bytes 18874384 | tf_op jit(solution)/shard_map/all_gather | solution.py:419
  795.7 14.1 %place.5 = f32[576,24576]{1,0:T(8,128)} custom-call(f32[64,576,128]{2,1,0:T(8,128)} %all-gather.8.cloned.1.call-done.refs_0_, f32[576,24576]{1,0:T(8,128)} %place.4.refs_1_), custom_call_target="tpu_custom_call", output_to_operand_aliasing={{}: (1, {})} | custom-call | flops 4718592 | bytes 37748736 | tf_op jit(solution)/shard_map/place/pallas_call | solution.py:352
  (10 shorter events, 0.1 us)
Async XLA Ops:
  7.2 149.0 %all-gather.14.cloned.1.call-start = ((), (), s32[]{:S(2)}) async-start(), calls=%async_computation.6 | async-start | bytes 11796480 | tf_op jit(solution)/shard_map/all_gather | solution.py:386
  12.1 306.8 %reduce-scatter.14.cloned.1.call-start = ((), (), s32[]{:S(2)}) async-start(), calls=%async_computation.9 | async-start | bytes 5013504
  218.9 158.1 %reduce-scatter.12.cloned.1.call-start = ((), (), s32[]{:S(2)}) async-start(), calls=%async_computation.8 | async-start | bytes 5013504
  268.7 190.0 %reduce-scatter.10.cloned.1.call-start = ((), (), s32[]{:S(2)}) async-start(), calls=%async_computation.7 | async-start | bytes 5013504
  318.8 349.1 %all-gather.12.cloned.1.call-start = ((), (), s32[]{:S(2)}) async-start(), calls=%async_computation.5 | async-start | bytes 19169280 | tf_op jit(solution)/shard_map/all_gather | solution.py:419
  319.4 364.6 %all-gather.10.cloned.1.call-start = ((), (), s32[]{:S(2)}) async-start(), calls=%async_computation.4 | async-start | bytes 19169280 | tf_op jit(solution)/shard_map/all_gather | solution.py:419
  377.0 418.6 %all-gather.8.cloned.1.call-start = ((), (), s32[]{:S(2)}) async-start(), calls=%async_computation.3 | async-start | bytes 19169280 | tf_op jit(solution)/shard_map/all_gather | solution.py:419
  587.4 4.5 collective-permute-start
  591.9 1.4 copy-start
Sparse Core Ops, SparseCore 0:
  12.2 96.3 all-gather.13
  219.0 76.1 reduce-scatter.13
  298.5 78.4 reduce-scatter.11
  380.2 78.4 reduce-scatter.9
  461.3 108.9 all-gather.11
  573.0 110.9 all-gather.9
  686.7 108.9 all-gather.7

commit v2 on v1

v2 whole, which is shorter than its diff:
```python
import jax
import jax.numpy as jnp
from jax import lax
from jax.experimental import pallas as pl
from jax.experimental.pallas import tpu as pltpu
from jax.sharding import Mesh, PartitionSpec as P

SOFT_CAP = 30.0
INV_CAP = 1.0 / SOFT_CAP
CAP_LOG2E = SOFT_CAP * 1.4426950408889634
LANES = 128
RING = 4
VMEM_LIMIT = 60 * 1024 * 1024
F32 = jnp.float32
BF16 = jnp.bfloat16
FAR = -(2 ** 22)
MESH_ID = pl.DeviceIdType.MESH
AXES = ('z', 'y', 'x', 'core')
SIZES = {'z': RING, 'y': RING, 'x': RING, 'core': 2}


def dot_f32(a, b, dims):
    return lax.dot_general(a, b, (dims, ((), ())), preferred_element_type=F32)


def grid_params(**kw):
    return pltpu.CompilerParams(
        dimension_semantics=("arbitrary",), vmem_limit_bytes=VMEM_LIMIT, **kw)


def peer(**shift):
    place = []
    for axis in AXES:
        here = lax.axis_index(axis)
        if axis in shift:
            here = lax.rem(here + shift[axis], SIZES[axis])
        place.append(here)
    return tuple(place)


def send(src, dst, send_sem, recv_sem, where):
    return pltpu.make_async_remote_copy(
        src, dst, send_sem, recv_sem, device_id=where, device_id_type=MESH_ID)


def meet(peers):
    barrier = pltpu.get_barrier_semaphore()
    for where in peers:
        pl.semaphore_signal(barrier, inc=1, device_id=where, device_id_type=MESH_ID)
    pl.semaphore_wait(barrier, len(peers))


def sum_slots(slot_ref, k, axis):
    total = slot_ref[k, 0]
    for i in range(1, SIZES[axis]):
        total = total + slot_ref[k, i]
    return total


def norm_body(ht_ref, w1_ref, xt_ref, xb_ref):
    h = ht_ref[...].astype(F32)
    inv_rms = lax.rsqrt(jnp.mean(h * h, axis=0, keepdims=True) + 1e-6)
    xt = h * inv_rms * jnp.broadcast_to(w1_ref[:, :1], h.shape)
    xt_ref[0] = xt
    xb_ref[...] = xt.T.astype(BF16)


def norm_rows(ht, w1):
    dim, tokens = ht.shape
    tb = tokens // 2
    return pl.pallas_call(
        norm_body,
        grid=(2,),
        in_specs=[
            pl.BlockSpec((dim, tb), lambda i: (0, i)),
            pl.BlockSpec((dim, LANES), lambda i: (0, 0)),
        ],
        out_specs=[
            pl.BlockSpec((1, dim, tb), lambda i: (i, 0, 0)),
            pl.BlockSpec((tb, dim), lambda i: (i, 0)),
        ],
        out_shape=[
            jax.ShapeDtypeStruct((2, dim, tb), F32),
            jax.ShapeDtypeStruct((tokens, dim), BF16),
        ],
        compiler_params=grid_params(),
        cost_estimate=pl.CostEstimate(
            flops=10 * dim * tokens, bytes_accessed=8 * dim * tokens, transcendentals=0),
        name="norm",
    )(ht, w1)


def norm_back_body(ht_ref, w1_ref, g0_ref, g1_ref, loss_ref, dh_ref, sum_ref,
                   dw_ref, cur_ref, slot_ref, send_sem, recv_sem):
    step = pl.program_id(0)
    dim, tb = ht_ref.shape
    h = ht_ref[...].astype(F32)
    inv_rms = lax.rsqrt(jnp.mean(h * h, axis=0, keepdims=True) + 1e-6)
    n = h * inv_rms
    g = g0_ref[...] + g1_ref[...]
    gn = g * n

    @pl.when(step == 0)
    def _():
        dw_ref[...] = jnp.zeros_like(dw_ref)

    part = dw_ref[...]
    for j in range(tb // LANES):
        part = part + gn[:, j * LANES:(j + 1) * LANES]
    dw_ref[...] = part
    w1 = jnp.broadcast_to(w1_ref[:, :1], h.shape)
    inner = jnp.mean(gn * w1, axis=0, keepdims=True)
    dh_ref[...] = ((g * w1 - n * inner) * inv_rms).astype(BF16)

    @pl.when(step == pl.num_programs(0) - 1)
    def _():
        cur_ref[0] = jnp.zeros_like(cur_ref[0])
        cur_ref[0, 0:1, 0:dim] = jnp.sum(dw_ref[...].T, axis=0, keepdims=True)
        cur_ref[0, 1:2, 0:LANES] = loss_ref[0:1, :]
        meet([peer(**{axis: r}) for axis in ('x', 'y', 'z') for r in range(1, SIZES[axis])])
        for k, axis in enumerate(('x', 'y', 'z')):
            me = lax.axis_index(axis)
            copies = []
            for r in range(1, SIZES[axis]):
                copies.append(send(cur_ref.at[k], slot_ref.at[k, me], send_sem.at[k, r - 1],
                                   recv_sem.at[k, r - 1], peer(**{axis: r})))
                copies[-1].start()
            slot_ref[k, me] = cur_ref[k]
            for copy in copies:
                copy.wait()
            cur_ref[k + 1] = sum_slots(slot_ref, k, axis)
        sum_ref[...] = cur_ref[3]


def norm_back(ht, w1, g0, g1, loss_tile):
    dim, tokens = ht.shape
    tb = tokens // 2
    width = -(-dim // LANES) * LANES
    return pl.pallas_call(
        norm_back_body,
        grid=(2,),
        in_specs=[
            pl.BlockSpec((dim, tb), lambda i: (0, i)),
            pl.BlockSpec((dim, LANES), lambda i: (0, 0)),
            pl.BlockSpec((dim, tb), lambda i: (0, i)),
            pl.BlockSpec((dim, tb), lambda i: (0, i)),
            pl.BlockSpec((8, LANES), lambda i: (0, 0)),
        ],
        out_specs=[
            pl.BlockSpec((dim, tb), lambda i: (0, i)),
            pl.BlockSpec((8, width), lambda i: (0, 0)),
        ],
        out_shape=[
            jax.ShapeDtypeStruct((dim, tokens), BF16),
            jax.ShapeDtypeStruct((8, width), F32),
        ],
        scratch_shapes=[
            pltpu.VMEM((dim, LANES), F32),
            pltpu.VMEM((4, 8, width), F32),
            pltpu.VMEM((3, RING, 8, width), F32),
            pltpu.SemaphoreType.DMA((3, 3)),
            pltpu.SemaphoreType.DMA((3, 3)),
        ],
        compiler_params=grid_params(collective_id=3, has_side_effects=True),
        cost_estimate=pl.CostEstimate(
            flops=20 * dim * tokens, bytes_accessed=12 * dim * tokens, transcendentals=0),
        name="norm_back",
    )(ht, w1, g0, g1, loss_tile)


def fwd_body(tb, early, late, x_ref, lab_ref, mask_ref, row_ref, e_ref, xt_ref,
             xg_ref, stat_ref, count_ref,
             z_ref, p_ref, pay_ref, cnt_ref, slot_ref,
             ring_send, ring_recv, half_send, half_recv, die_send, die_recv,
             cnt_send, cnt_recv, stat_send, stat_recv, own_sem):
    step = pl.program_id(0)
    last = pl.num_programs(0) - 1
    tokens = x_ref.shape[0]
    bv = e_ref.shape[1]
    dim = e_ref.shape[0]
    cut = dim // 16 * 8
    core = lax.axis_index('core')
    right, left, across = peer(x=1), peer(x=RING - 1), peer(core=1)

    to_right = send(xt_ref.at[core], xg_ref.at[0, core], ring_send.at[0], ring_recv.at[0], right)
    to_left = send(xt_ref.at[core], xg_ref.at[2, core], ring_send.at[1], ring_recv.at[1], left)
    on_right = send(xg_ref.at[0, core, pl.ds(0, cut)], xg_ref.at[1, core, pl.ds(0, cut)],
                    half_send.at[0], half_recv.at[0], right)
    on_left = send(xg_ref.at[2, core, pl.ds(cut, dim - cut)],
                   xg_ref.at[1, core, pl.ds(cut, dim - cut)],
                   half_send.at[1], half_recv.at[1], left)
    over = [send(xg_ref.at[r, core], xg_ref.at[r, core], die_send.at[r], die_recv.at[r], across)
            for r in range(3)]

    def count_copies(k, axis):
        me = lax.axis_index(axis)
        return [send(cnt_ref.at[k], slot_ref.at[k, me], cnt_send.at[k, r - 1],
                     cnt_recv.at[k, r - 1], peer(**{axis: r})) for r in range(1, SIZES[axis])]

    def count_sum(k, axis):
        for copy in count_copies(k, axis):
            copy.wait()
        slot_ref[k, lax.axis_index(axis)] = cnt_ref[k]
        cnt_ref[k + 1] = sum_slots(slot_ref, k, axis)

    @pl.when(step == 0)
    def _():
        z_ref[...] = jnp.zeros_like(z_ref)
        p_ref[...] = jnp.zeros_like(p_ref)
        cnt_ref[0] = jnp.full(cnt_ref.shape[1:], jnp.sum(mask_ref[...]), F32)
        meet([peer(**{axis: r}) for axis in ('y', 'z') for r in range(1, SIZES[axis])]
             + [peer(x=r, core=c) for r in (1, 2, 3) for c in (0, 1)] + [across])
        to_right.start()
        to_left.start()
        for copy in count_copies(0, 'x'):
            copy.start()

    @pl.when(step == 4)
    def _():
        count_sum(0, 'x')
        for copy in count_copies(1, 'y'):
            copy.start()

    @pl.when(step == 8)
    def _():
        count_sum(1, 'y')
        for copy in count_copies(2, 'z'):
            copy.start()

    @pl.when(step == 12)
    def _():
        count_sum(2, 'z')
        count_ref[...] = cnt_ref[3]

    @pl.when(step == early)
    def _():
        to_right.wait()
        to_left.wait()
        on_right.start()
        on_left.start()
        over[0].start()
        over[2].start()

    @pl.when(step == late)
    def _():
        on_right.wait()
        on_left.wait()
        over[1].start()

    lane = lax.broadcasted_iota(jnp.int32, (tb, LANES), 1)

    def block(i, carry):
        rows = pl.ds(pl.multiple_of(i * tb, tb), tb)
        z = dot_f32(x_ref[rows, :], e_ref[...], ((1,), (0,)))
        lab = lab_ref[rows, :] - step * bv
        zsum = z_ref[rows, :]
        psum = p_ref[rows, :]
        for j in range(bv // LANES):
            t = jnp.tanh(z[:, j * LANES:(j + 1) * LANES] * INV_CAP)
            zsum = zsum + jnp.exp2(t * CAP_LOG2E)
            psum = jnp.where(lab == lane + j * LANES, t, psum)
        z_ref[rows, :] = zsum
        p_ref[rows, :] = psum
        return carry

    lax.fori_loop(0, tokens // tb, block, 0, unroll=True)

    @pl.when(step == last)
    def _():
        pay_ref[0:1, :] = jnp.sum(z_ref[...].T, axis=0, keepdims=True)
        pay_ref[1:2, :] = jnp.sum(p_ref[...].T, axis=0, keepdims=True)
        pay_ref[2:3, :] = row_ref[...]
        pay_ref[3:8, :] = jnp.zeros((5, tokens), F32)
        own = pltpu.make_async_copy(pay_ref, stat_ref.at[0, core], own_sem)
        own.start()
        copies = [send(pay_ref, stat_ref.at[0, core], stat_send.at[0], stat_recv.at[0], across)]
        for r in (1, 2, 3):
            for c in (0, 1):
                k = 2 * r - 1 + c
                copies.append(send(pay_ref, stat_ref.at[r, core], stat_send.at[k],
                                   stat_recv.at[k], peer(x=r, core=c)))
        for copy in copies:
            copy.start()
        for copy in over:
            copy.wait()
        own.wait()
        for copy in copies:
            copy.wait()


def forward(x, lab_rep, mask_tile, lab_row, et, xt, bv=512, tb=256):
    tokens, dim = x.shape
    vocab = et.shape[1]
    tb = min(tb, tokens)
    steps = vocab // bv
    early, late = max(13, steps * 25 // 48), max(14, steps * 38 // 48)
    anyspace = pl.BlockSpec(memory_space=pl.ANY)
    sem = pltpu.SemaphoreType.DMA
    return pl.pallas_call(
        lambda *refs: fwd_body(tb, early, late, *refs),
        grid=(steps,),
        in_specs=[
            pl.BlockSpec((tokens, dim), lambda i: (0, 0)),
            pl.BlockSpec((tokens, LANES), lambda i: (0, 0)),
            pl.BlockSpec((8, tokens // 8), lambda i: (0, 0)),
            pl.BlockSpec((1, tokens), lambda i: (0, 0)),
            pl.BlockSpec((dim, bv), lambda i: (0, i)),
            anyspace,
        ],
        out_specs=[anyspace, anyspace, pl.BlockSpec((8, LANES), lambda i: (0, 0))],
        out_shape=[
            jax.ShapeDtypeStruct((RING - 1, 2, dim, tokens // 2), F32),
            jax.ShapeDtypeStruct((RING, 2, 8, tokens), F32),
            jax.ShapeDtypeStruct((8, LANES), F32),
        ],
        scratch_shapes=[
            pltpu.VMEM((tokens, LANES), F32),
            pltpu.VMEM((tokens, LANES), F32),
            pltpu.VMEM((8, tokens), F32),
            pltpu.VMEM((4, 8, LANES), F32),
            pltpu.VMEM((3, RING, 8, LANES), F32),
            sem((2,)), sem((2,)), sem((2,)), sem((2,)), sem((3,)), sem((3,)),
            sem((3, 3)), sem((3, 3)), sem((7,)), sem((7,)), sem,
        ],
        compiler_params=grid_params(collective_id=1, has_side_effects=True),
        cost_estimate=pl.CostEstimate(
            flops=2 * tokens * dim * vocab, bytes_accessed=2 * dim * vocab,
            transcendentals=2 * tokens * vocab),
        name="fwd",
    )(x, lab_rep, mask_tile, lab_row, et, xt)


def prep_body(cnt_ref, own_ref, xg_ref, stat_ref, xb_ref, xt_ref, scale_ref, lab_ref, loss_ref):
    r = pl.program_id(0)
    _, dim, half = own_ref.shape
    inv_count = cnt_ref[0]
    tail = dim % LANES

    def store(x_ref):
        for side in range(2):
            v = (own_ref[side] if x_ref is own_ref else x_ref[0, side])
            vt = v.T.astype(BF16)
            vb = v.astype(BF16)
            rows = pl.ds(side * half, half)
            for k in range(dim // LANES):
                xb_ref[k, rows, :] = vt[:, k * LANES:(k + 1) * LANES]
            if tail:
                xb_ref[dim // LANES, rows, :] = jnp.concatenate(
                    [vt[:, dim - tail:], jnp.zeros((half, LANES - tail), BF16)], axis=1)
            for k in range(half // LANES):
                xt_ref[side * (half // LANES) + k] = vb[:, k * LANES:(k + 1) * LANES]

    @pl.when(r == 0)
    def _():
        store(own_ref)

    @pl.when(r != 0)
    def _():
        store(xg_ref)

    row_sum = stat_ref[0, 0, 0:1, :] + stat_ref[0, 1, 0:1, :]
    label = stat_ref[0, 0, 2:3, :]
    live = label >= 0.0
    scale = jnp.where(live, inv_count, 0.0) / row_sum
    for k in range(2 * half // LANES):
        cols = slice(k * LANES, (k + 1) * LANES)
        scale_ref[cols, :] = jnp.broadcast_to(scale[:, cols], (LANES, LANES)).T
        lab_ref[cols, :] = jnp.broadcast_to(label[:, cols], (LANES, LANES)).T.astype(jnp.int32)

    @pl.when(r == 0)
    def _():
        picked = (stat_ref[0, 0, 1:2, :] + stat_ref[0, 1, 1:2, :]) * SOFT_CAP
        loss = jnp.where(live, jnp.log(row_sum) - picked, 0.0)
        loss_ref[...] = jnp.full((8, LANES), jnp.sum(loss), F32)


def prep(inv_count, xt_own, xg, stat):
    _, dim, half = xt_own.shape
    tokens = 2 * half
    slabs = -(-dim // LANES)
    per = tokens // LANES
    return pl.pallas_call(
        prep_body,
        grid=(RING,),
        in_specs=[
            pl.BlockSpec(memory_space=pltpu.SMEM),
            pl.BlockSpec((2, dim, half), lambda i: (0, 0, 0)),
            pl.BlockSpec((1, 2, dim, half), lambda i: (jnp.maximum(i - 1, 0), 0, 0, 0)),
            pl.BlockSpec((1, 2, 8, tokens), lambda i: (i, 0, 0, 0)),
        ],
        out_specs=[
            pl.BlockSpec((slabs, tokens, LANES), lambda i: (0, i, 0)),
            pl.BlockSpec((per, dim, LANES), lambda i: (i, 0, 0)),
            pl.BlockSpec((tokens, LANES), lambda i: (i, 0)),
            pl.BlockSpec((tokens, LANES), lambda i: (i, 0)),
            pl.BlockSpec((8, LANES), lambda i: (0, 0)),
        ],
        out_shape=[
            jax.ShapeDtypeStruct((slabs, RING * tokens, LANES), BF16),
            jax.ShapeDtypeStruct((RING * per, dim, LANES), BF16),
            jax.ShapeDtypeStruct((RING * tokens, LANES), F32),
            jax.ShapeDtypeStruct((RING * tokens, LANES), jnp.int32),
            jax.ShapeDtypeStruct((8, LANES), F32),
        ],
        compiler_params=grid_params(),
        cost_estimate=pl.CostEstimate(
            flops=40 * dim * tokens, bytes_accessed=32 * dim * tokens, transcendentals=0),
        name="prep",
    )(inv_count, xt_own, xg, stat)


def grad_tile(z, scale, lab, vid, inv_count):
    t = jnp.tanh(z * INV_CAP)
    p = jnp.exp2(t * CAP_LOG2E) * scale
    p = jnp.where(lab == vid, p - inv_count, p)
    return (p * (1.0 - t * t)).astype(BF16)


def table_body(first, n_chunks, tb, cnt_ref, off_ref, xb_ref, xt_ref, scale_ref, lab_ref, et_ref,
               out_ref, ebuf, ga_ref, gb_ref, tiles, part_in, tile_in, bpart_in, btile_in,
               esem, psend, precv, tsend, trecv, bpsend, bprecv, btsend, btrecv):
    slabs, group_tokens, _ = xb_ref.shape
    dim = xt_ref.shape[1]
    blocks = group_tokens // tb
    cut = dim // 16 * 8
    rest = dim - cut
    units = 8 * n_chunks
    inv_count = cnt_ref[0]
    vocab_off = off_ref[0]
    zi, yi, xi = (lax.axis_index(a) for a in ('z', 'y', 'x'))
    lane = lax.broadcasted_iota(jnp.int32, (tb, LANES), 1)

    def shifted(odd, da, db):
        return peer(z=db + odd * (da - db), y=da + odd * (db - da))

    def tile_index(u, j):
        k = u // 8
        odd = lax.rem(first + k, 2)
        s = lax.rem(u, 8) // 2
        half = lax.rem(u, 2)
        rb = lax.rem(2 + 3 * s + 3 * (s * (s - 1) // 2), 4)
        ra = 2 + half - j * (1 + 2 * half)
        dz, dy = rb + odd * (ra - rb), ra + odd * (rb - ra)
        return (((first + k) * 4 + lax.rem(zi + dz, 4)) * 4 + lax.rem(yi + dy, 4)) * 4 + xi

    def fetch(u, j):
        cols = pl.ds(pl.multiple_of(tile_index(u, j) * LANES, LANES), LANES)
        slot = lax.rem(u, 2)
        return pltpu.make_async_copy(
            et_ref.at[:, cols], ebuf.at[slot, j, pl.ds(0, dim)], esem.at[slot, j])

    def part_copies(q):
        odd = lax.rem(first + q // 4, 2)
        return (send(tiles.at[q, 0, pl.ds(0, cut)], part_in.at[q, 0, pl.ds(0, cut)],
                     psend.at[q, 0], precv.at[q, 0], shifted(odd, 1, 0)),
                send(tiles.at[q, 0, pl.ds(cut, rest)], part_in.at[q, 1, pl.ds(0, rest)],
                     psend.at[q, 1], precv.at[q, 1], shifted(odd, 3, 0)))

    def tile_copies(q):
        odd = lax.rem(first + q // 4, 2)
        return (send(tiles.at[q, 1], tile_in.at[q, 0], tsend.at[q, 0], trecv.at[q, 0],
                     shifted(odd, 1, 0)),
                send(tiles.at[q, 2], tile_in.at[q, 1], tsend.at[q, 1], trecv.at[q, 1],
                     shifted(odd, 3, 0)))

    def bpart_copies(k):
        odd = lax.rem(first + k, 2)
        return (send(tiles.at[4 * k, 3, pl.ds(0, cut)], bpart_in.at[k, 0, pl.ds(0, cut)],
                     bpsend.at[k, 0], bprecv.at[k, 0], shifted(odd, 0, 1)),
                send(tiles.at[4 * k, 3, pl.ds(cut, rest)], bpart_in.at[k, 1, pl.ds(0, rest)],
                     bpsend.at[k, 1], bprecv.at[k, 1], shifted(odd, 0, 3)))

    def btile_copies(k):
        odd = lax.rem(first + k, 2)
        return (send(tiles.at[4 * k + 1, 3], btile_in.at[k, 0], btsend.at[k, 0], btrecv.at[k, 0],
                     shifted(odd, 0, 1)),
                send(tiles.at[4 * k + 2, 3], btile_in.at[k, 1], btsend.at[k, 1], btrecv.at[k, 1],
                     shifted(odd, 0, 3)))

    def start(copies):
        for copy in copies:
            copy.start()

    def arrive(copies):
        for copy in copies:
            copy.wait_recv()

    def close_slab(q):
        arrive(tile_copies(q))
        tiles[q, 3] = tiles[q, 3] + (tile_in[q, 0] + tile_in[q, 1])

    def close_chunk(k):
        close_slab(4 * k + 3)
        arrive(btile_copies(k))
        out_ref[k] = tiles[4 * k + 3, 3] + (btile_in[k, 0] + btile_in[k, 1])

    if slabs * LANES > dim:
        for slot in range(2):
            for j in range(2):
                ebuf[slot, j, dim:, :] = jnp.zeros((slabs * LANES - dim, LANES), BF16)
    for j in range(2):
        fetch(0, j).start()
    meet([peer(y=1), peer(y=3), peer(z=1), peer(z=3)])

    def unit(u, carry):
        slot = lax.rem(u, 2)
        q = u // 2
        k = u // 8
        s = lax.rem(q, 4)
        half = lax.rem(u, 2)
        for j in range(2):
            fetch(u, j).wait()

        @pl.when(u + 1 < units)
        def _():
            for j in range(2):
                fetch(u + 1, j).start()

        bases = [tile_index(u, j) * LANES + vocab_off for j in range(2)]

        def rows_of(i):
            return pl.ds(pl.multiple_of(i * tb, tb), tb)

        def grads(i, g_ref):
            rows = rows_of(i)
            x = jnp.concatenate([xb_ref[n, rows, :] for n in range(slabs)], axis=1)
            e = jnp.concatenate([ebuf[slot, 0], ebuf[slot, 1]], axis=1)
            z = dot_f32(x, e, ((1,), (0,)))
            lab = lab_ref[rows, :]
            scale = scale_ref[rows, :]
            for j in range(2):
                g_ref[j] = grad_tile(z[:, j * LANES:(j + 1) * LANES], scale, lab - bases[j], lane,
                                     inv_count)

        def product(i, g_ref):
            n = tb // LANES
            x = jnp.concatenate([xt_ref[i * n + m] for m in range(n)], axis=1)
            g = jnp.concatenate([g_ref[0], g_ref[1]], axis=1)
            return dot_f32(x, g, ((1,), (0,)))

        def add(i, g_ref):
            part = product(i, g_ref)
            for j in range(2):
                tiles[q, 2 * half + j] += part[:, j * LANES:(j + 1) * LANES]

        grads(0, ga_ref)
        grads(1, gb_ref)
        part = product(0, ga_ref)
        for j in range(2):
            tiles[q, 2 * half + j] = part[:, j * LANES:(j + 1) * LANES]

        def pair(i, c):
            grads(2 * i, ga_ref)
            add(2 * i - 1, gb_ref)
            grads(2 * i + 1, gb_ref)
            add(2 * i, ga_ref)
            return c

        lax.fori_loop(1, blocks // 2, pair, 0)
        add(blocks - 1, gb_ref)

        @pl.when(half == 0)
        def _():
            @pl.when((s == 1) & (k > 0))
            def _():
                close_chunk(k - 1)

            start(part_copies(q))

        @pl.when(half == 1)
        def _():
            arrive(part_copies(q))
            tiles[q, 1, 0:cut, :] += part_in[q, 0, 0:cut, :]
            tiles[q, 2, cut:dim, :] += part_in[q, 1, 0:rest, :]

            @pl.when(s >= 1)
            def _():
                close_slab(q - 1)

            start(tile_copies(q))

            @pl.when(s == 1)
            def _():
                start(bpart_copies(k))

            @pl.when(s == 3)
            def _():
                arrive(bpart_copies(k))
                tiles[4 * k + 1, 3, 0:cut, :] += bpart_in[k, 0, 0:cut, :]
                tiles[4 * k + 2, 3, cut:dim, :] += bpart_in[k, 1, 0:rest, :]
                start(btile_copies(k))
        return carry

    lax.fori_loop(0, units, unit, 0)
    close_chunk(n_chunks - 1)

    def sent(q, carry):
        for copy in part_copies(q) + tile_copies(q):
            copy.wait_send()
        return carry

    lax.fori_loop(0, 4 * n_chunks, sent, 0)
    for k in range(n_chunks):
        for copy in bpart_copies(k) + btile_copies(k):
            copy.wait_send()


def table_chunks(first, n_chunks, inv_count, vocab_off, xb, xt, scale, lab, et, ident, tb=512):
    slabs, group_tokens, _ = xb.shape
    dim = xt.shape[1]
    tb = min(tb, group_tokens // 4)
    part = max(dim // 16 * 8, dim - dim // 16 * 8)
    smem = pl.BlockSpec(memory_space=pltpu.SMEM)
    vmem = pl.BlockSpec(memory_space=pltpu.VMEM)
    n_slabs = 4 * n_chunks
    sem = pltpu.SemaphoreType.DMA
    tokens = n_chunks * 16 * LANES * group_tokens
    return pl.pallas_call(
        lambda *refs: table_body(first, n_chunks, tb, *refs),
        in_specs=[smem, smem, vmem, vmem, vmem, vmem, pl.BlockSpec(memory_space=pl.ANY)],
        out_specs=vmem,
        out_shape=jax.ShapeDtypeStruct((n_chunks, dim, LANES), F32),
        scratch_shapes=[
            pltpu.VMEM((2, 2, slabs * LANES, LANES), BF16),
            pltpu.VMEM((2, tb, LANES), BF16),
            pltpu.VMEM((2, tb, LANES), BF16),
            pltpu.VMEM((n_slabs, 4, dim, LANES), F32),
            pltpu.VMEM((n_slabs, 2, part, LANES), F32),
            pltpu.VMEM((n_slabs, 2, dim, LANES), F32),
            pltpu.VMEM((n_chunks, 2, part, LANES), F32),
            pltpu.VMEM((n_chunks, 2, dim, LANES), F32),
            sem((2, 2)), sem((n_slabs, 2)), sem((n_slabs, 2)), sem((n_slabs, 2)),
            sem((n_slabs, 2)), sem((n_chunks, 2)), sem((n_chunks, 2)), sem((n_chunks, 2)),
            sem((n_chunks, 2)),
        ],
        compiler_params=pltpu.CompilerParams(
            collective_id=ident, has_side_effects=True, vmem_limit_bytes=VMEM_LIMIT),
        cost_estimate=pl.CostEstimate(
            flops=4 * dim * tokens, bytes_accessed=4 * dim * group_tokens,
            transcendentals=2 * tokens),
        name="table_grad",
    )(inv_count, vocab_off, xb, xt, scale, lab, et)


def rows_body(tb, cnt_ref, off_ref, x_ref, scale_ref, lab_ref, e_ref, out_ref, g_ref):
    step = pl.program_id(0)
    tokens = x_ref.shape[0]
    bv = e_ref.shape[1]
    inv_count = cnt_ref[0]
    base = step * bv + off_ref[0]

    @pl.when(step == 0)
    def _():
        out_ref[...] = jnp.zeros_like(out_ref)

    lane = lax.broadcasted_iota(jnp.int32, (tb, LANES), 1)

    def block(i, carry):
        rows = pl.ds(pl.multiple_of(i * tb, tb), tb)
        z = dot_f32(x_ref[rows, :], e_ref[...], ((1,), (0,)))
        lab = lab_ref[rows, :] - base
        scale = scale_ref[rows, :]
        for j in range(bv // LANES):
            g_ref[:, j * LANES:(j + 1) * LANES] = grad_tile(
                z[:, j * LANES:(j + 1) * LANES], scale, lab, lane + j * LANES, inv_count)
        out_ref[:, rows] += dot_f32(e_ref[...], g_ref[...], ((1,), (1,)))
        return carry

    lax.fori_loop(0, tokens // tb, block, 0)


def rows_grad(inv_count, vocab_off, x, scale, lab, et, bv=1024, tb=256):
    tokens, dim = x.shape
    vocab = et.shape[1]
    tb = min(tb, tokens)
    smem = pl.BlockSpec(memory_space=pltpu.SMEM)
    return pl.pallas_call(
        lambda *refs: rows_body(tb, *refs),
        grid=(vocab // bv,),
        in_specs=[
            smem,
            smem,
            pl.BlockSpec((tokens, dim), lambda i: (0, 0)),
            pl.BlockSpec((tokens, LANES), lambda i: (0, 0)),
            pl.BlockSpec((tokens, LANES), lambda i: (0, 0)),
            pl.BlockSpec((dim, bv), lambda i: (0, i)),
        ],
        out_specs=pl.BlockSpec((dim, tokens), lambda i: (0, 0)),
        out_shape=jax.ShapeDtypeStruct((dim, tokens), F32),
        scratch_shapes=[pltpu.VMEM((tb, bv), BF16)],
        compiler_params=grid_params(),
        cost_estimate=pl.CostEstimate(
            flops=4 * tokens * dim * vocab, bytes_accessed=2 * dim * vocab,
            transcendentals=2 * tokens * vocab),
        name="rows_grad",
    )(inv_count, vocab_off, x, scale, lab, et)


def place_body(n, src_ref, *refs):
    out_ref = refs[-1]
    for k in range(n):
        out_ref[:, k * LANES:(k + 1) * LANES] = src_ref[k]


def place_chunk(c, gathered, table, vocab):
    n_dev, dim, _ = gathered.shape
    rows = 96 if dim % 96 == 0 else dim
    in_specs = [pl.BlockSpec((n_dev, rows, LANES), lambda i: (0, i, 0))]
    args = [gathered]
    alias = {}
    if table is not None:
        in_specs.append(pl.BlockSpec(memory_space=pl.ANY))
        args.append(table)
        alias = {1: 0}
    return pl.pallas_call(
        lambda *refs: place_body(n_dev, *refs),
        grid=(dim // rows,),
        in_specs=in_specs,
        out_specs=pl.BlockSpec((rows, n_dev * LANES), lambda i: (i, c)),
        out_shape=jax.ShapeDtypeStruct((dim, vocab), F32),
        input_output_aliases=alias,
        compiler_params=grid_params(),
        cost_estimate=pl.CostEstimate(
            flops=n_dev * dim * LANES, bytes_accessed=8 * n_dev * dim * LANES, transcendentals=0),
        name="place",
    )(*args)


def solution(mesh):
    grid_mesh = Mesh(mesh.devices.reshape(RING, RING, RING, 2), AXES)
    dp = ('z', 'y', 'x')

    def local_step(hidden, norm_w, embed_table, labels, loss_mask):
        batch_rows, seq_len, dim = hidden.shape
        vocab = embed_table.shape[0]
        tokens = batch_rows * seq_len
        et = embed_table.T
        ht = hidden.reshape(tokens, dim).T
        w1 = jnp.broadcast_to((1.0 + norm_w.astype(F32))[:, None], (dim, LANES))
        mask_row = loss_mask.reshape(1, tokens)
        lab_row = labels.reshape(1, tokens)
        core = lax.axis_index('core')

        xt_own, xb_own = norm_rows(ht, w1)
        lab_rep = jnp.broadcast_to((lab_row.reshape(tokens) - core * vocab)[:, None], (tokens, LANES))
        lab_live = jnp.where(mask_row > 0, lab_row, FAR).astype(F32)
        xg, stat, count = forward(
            xb_own, lab_rep, mask_row.reshape(8, tokens // 8).astype(F32), lab_live, et, xt_own)
        inv_count = (1.0 / jnp.maximum(count[0, 0], 1.0)).reshape(1)
        vocab_off = (core * vocab).astype(jnp.int32).reshape(1)
        xb, xt, scale, lab, loss_tile = prep(inv_count, xt_own, xg, stat)

        n_chunks = vocab // (64 * LANES)
        runs = [(0, 1), (1, n_chunks - 1)] if n_chunks > 1 else [(0, 1)]
        mine = []
        for n, (first, many) in enumerate(runs):
            got = table_chunks(first, many, inv_count, vocab_off, xb, xt, scale, lab, et, 4 + n)
            mine += [got[k] for k in range(many)]
        table = None
        for c in range(n_chunks):
            gathered = lax.all_gather(mine[c], dp, axis=0)
            table = place_chunk(c, gathered, table, vocab)

        xb_late, _ = lax.optimization_barrier((xb_own, mine[-1]))
        gxt = rows_grad(inv_count, vocab_off, xb_late, scale[:tokens], lab[:tokens], et)
        dht, sums = norm_back(
            ht, w1, gxt, lax.ppermute(gxt, 'core', [(0, 1), (1, 0)]), loss_tile)
        return (sums[1, 0] * inv_count[0], dht.T.reshape(batch_rows, seq_len, dim),
                sums[0, :dim], table.T)

    return jax.shard_map(
        local_step, mesh=grid_mesh,
        in_specs=(P(dp, None, None), P(None), P('core', None), P(dp, None), P(dp, None)),
        out_specs=(P(), P(dp, None, None), P(None), P('core', None)), check_vma=False)
```

time: 820 us -> 588 us (0.72)
  waiting for transfers between devices: 244 us -> 40.7 us
  blocking collectives: 150 us -> 0 us
  Pallas kernels: 389 us -> 514 us
    unnamed x10 -> x3, waiting for transfers between devices: 140 us -> 0.71 us
    psum x2 -> x0, blocking collectives: 137 us -> none  [the longest x1 70.1 us: local_step(): count = jnp.maximum(lax.psum(jnp.sum(mask_rows), every) * 0.5, 1.0)]
    pallas_call x7 -> x6, Pallas kernels: 221 us -> 345 us  [the longest x2 220 us: table_chunks(): pl.pallas_call(lambda *refs: table_body(first, n_chunks, tb, *refs), in_s...]
    all_gather x4 -> x3, waiting for transfers between devices: 99.7 us -> 35.5 us  [local_step(): gathered = lax.all_gather(mine[c], dp, axis=0)]
    all_gather x1 -> x0, blocking collectives: 12.8 us -> none  [local_step(): lax.all_gather(jnp.stack([jnp.sum(zpart, axis=1), jnp.sum(ppart, axis=1),...]
    slice x0 -> x6, local copies, waits for them, and re-layouts: none -> 9.38 us  [the longest x1 1.93 us: local_step(): mine += [got[k] for k in range(many)]]
  transfers between devices with their start and end apart: 8 -> 4, of which waited for: 5 -> 2; matrix products, arithmetic and copies ran while one was open for 1% -> 1% of each run, Pallas kernels for 38% -> 56%
where the time goes in v2:
time: 588 us; the launch traced here: 586 us
  Pallas kernels  514 us (87%)
  waiting for transfers between devices  40.7 us (7%)
  between operations  16.3 us (3%)
  local copies, waits for them, and re-layouts  13.7 us (2%)
    pallas_call x2, Pallas kernels, table_chunks(): pl.pallas_call(lambda *refs: table_body(first, n_chunks, tb, *refs), in_s...  220 us
    pallas_call x1, Pallas kernels, rows_grad(): pl.pallas_call(lambda *refs: rows_body(tb, *refs), grid=(vocab // bv,), i...  126 us
    pallas_call x1, Pallas kernels, forward(): pl.pallas_call(lambda *refs: fwd_body(tb, early, late, *refs), grid=(step...  92.2 us
    pallas_call x3, Pallas kernels, place_chunk(): pl.pallas_call(lambda *refs: place_body(n_dev, *refs), grid=(dim // rows,...  42.2 us
    all_gather x3, waiting for transfers between devices, local_step(): gathered = lax.all_gather(mine[c], dp, axis=0)  35.5 us
    pallas_call x1, Pallas kernels, norm_back(): pl.pallas_call(norm_back_body, grid=(2,), in_specs=[pl.BlockSpec((dim, tb...  18.8 us
  transfers between devices with their start and end apart: 4, of which 2 were waited for; matrix products, arithmetic and copies ran while one was open for 1% of the time, Pallas kernels for 56%

profile of v2, /device:TPU:0, one launch (start us, length us, event | category | flops | bytes accessed | tf_op | source)
XLA Modules:
  0.0 586.5 jit_solution(1651188271986324401)
XLA Ops:
  7.2 0.0 all-gather.8.cloned.1.call-start
  7.2 0.7 convert_add_fusion
  7.9 0.9 broadcast_in_dim.7.w1_ref
  8.8 3.4 norm.1
  12.2 1.4 fusion
  13.5 1.0 broadcast_in_dim.8.refs_1_
  14.5 92.2 %fwd.1 = (f32[3,2,576,512]{3,2,1,0:T(8,128)}, f32[4,2,8,1024]{3,2,1,0:T(8,128)}, f32[8,128]{1,0:T(8,128)}) custom-call(bf16[1024,576]{1,0:T(8,128)(2,1)} %get-tuple-element.16.refs_0_.refs_2_, s32[1024,128]{1,0:T(8,128)} %broadcast_in_dim.8.refs_1_, f32[8,128]{1,0:T(8,128)} %bitcast.18, f32[1,1024]{1,0:T(1,128)} %get-tuple-element.30.refs_3_, ...), custom_call_target="tpu_custom_call" | custom-call | flops 28991029248 | bytes 28311552 | tf_op jit(solution)/shard_map/fwd/pallas_call | solution.py:299
  106.7 1.2 slice.21
  108.6 10.8 %prep.1 = (bf16[5,4096,128]{2,1,0:T(8,128)(2,1)}, bf16[32,576,128]{2,1,0:T(8,128)(2,1)}, f32[4096,128]{1,0:T(8,128)}, s32[4096,128]{1,0:T(8,128)}, f32[8,128]{1,0:T(8,128)}) custom-call(f32[1]{0:T(128)} %bitcast.6.cnt_ref.refs_0_, f32[2,576,512]{2,1,0:T(8,128)} %get-tuple-element.17.refs_5_.own_ref, f32[3,2,576,512]{3,2,1,0:T(8,128)} %get-tuple-element.19.xg_ref, ...), custom_call_target="tpu_custom_call" | custom-call | flops 23592960 | bytes 18874368 | tf_op jit(solution)/shard_map/prep/pallas_call | solution.py:382
  119.4 63.0 %table_grad.3 = f32[1,576,128]{2,1,0:T(8,128)} custom-call(f32[1]{0:T(128)} %bitcast.6.cnt_ref.refs_0_, s32[1]{0:T(128)} %bitcast.7.refs_1_, bf16[5,4096,128]{2,1,0:T(8,128)(2,1)} %get-tuple-element.26.refs_2_, bf16[32,576,128]{2,1,0:T(8,128)(2,1)} %get-tuple-element.27.refs_3_, f32[4096,128]{1,0:T(8,128)} %get-tuple-element.21.refs_4_, ...), custom_call_target="tpu_custom_call" | custom-call | flops 19327352832 | bytes 9437184 | tf_op jit(solution)/shard_map/table_grad/pallas_call | solution.py:618
  182.4 0.0 all-gather.8.cloned.1.call-update
  182.4 0.0 all-gather.6.cloned.1.call-start
  182.5 157.3 %table_grad.2 = f32[2,576,128]{2,1,0:T(8,128)} custom-call(f32[1]{0:T(128)} %bitcast.6.cnt_ref.refs_0_, s32[1]{0:T(128)} %bitcast.7.refs_1_, bf16[5,4096,128]{2,1,0:T(8,128)(2,1)} %get-tuple-element.26.refs_2_, bf16[32,576,128]{2,1,0:T(8,128)(2,1)} %get-tuple-element.27.refs_3_, f32[4096,128]{1,0:T(8,128)} %get-tuple-element.21.refs_4_, ...), custom_call_target="tpu_custom_call" | custom-call | flops 38654705664 | bytes 9437184 | tf_op jit(solution)/shard_map/table_grad/pallas_call | solution.py:618
  339.8 1.9 fusion.1
  341.7 0.0 all-gather.6.cloned.1.call-update
  341.8 0.0 all-gather.4.cloned.1.call-start
  341.8 0.7 all-gather.4.cloned.1.call-update
  342.5 1.9 slice.22.refs_3_
  344.4 1.9 slice.23.refs_4_
  346.2 126.0 %rows_grad.1.g0_ref = f32[576,1024]{1,0:T(8,128)} custom-call(f32[1]{0:T(128)} %bitcast.6.cnt_ref.refs_0_, s32[1]{0:T(128)} %bitcast.7.refs_1_, bf16[1024,576]{1,0:T(8,128)(2,1)} %get-tuple-element.16.refs_0_.refs_2_, f32[1024,128]{1,0:T(8,128)} %slice.22.refs_3_, s32[1024,128]{1,0:T(8,128)} %slice.23.refs_4_, bf16[576,24576]{1,0:T(8,128)(2,1)} %bitcast.22), custom_call_target="tpu_custom_call" | custom-call | flops 57982058496 | bytes 28311552 | tf_op jit(solution)/shard_map/rows_grad/pallas_call | solution.py:677
  472.2 0.0 collective-permute-start
  472.2 4.5 collective-permute-done.g1_ref
  476.7 0.0 copy-start
  476.7 1.5 copy-done
  478.2 18.8 %norm_back.1 = (bf16[576,1024]{1,0:T(8,128)(2,1)}, f32[8,640]{1,0:T(8,128)}) custom-call(bf16[576,1024]{1,0:T(8,128)(2,1)} %bitcast.15, f32[576,128]{1,0:T(8,128)} %broadcast_in_dim.7.w1_ref, f32[576,1024]{1,0:T(8,128)} %rows_grad.1.g0_ref, f32[576,1024]{1,0:T(8,128)} %copy-done, f32[8,128]{1,0:T(8,128)} %get-tuple-element.23.loss_ref), custom_call_target="tpu_custom_call" | custom-call | flops 11796480 | bytes 7077888 | tf_op jit(solution)/shard_map/norm_back/pallas_call | solution.py:139
  497.0 1.2 slice.24
  498.8 1.3 slice_reduce_fusion
  500.2 0.0 all-gather.8.cloned.1.call-done.refs_0_
  500.2 14.1 %place.3.refs_1_ = f32[576,24576]{1,0:T(8,128)} custom-call(f32[64,576,128]{2,1,0:T(8,128)} %all-gather.8.cloned.1.call-done.refs_0_), custom_call_target="tpu_custom_call" | custom-call | flops 4718592 | bytes 37748736 | tf_op jit(solution)/shard_map/place/pallas_call | solution.py:715
  514.2 0.0 all-gather.6.cloned.1.call-done.refs_0_
  514.2 14.1 %place.4.refs_1_ = f32[576,24576]{1,0:T(8,128)} custom-call(f32[64,576,128]{2,1,0:T(8,128)} %all-gather.6.cloned.1.call-done.refs_0_, f32[576,24576]{1,0:T(8,128)} %place.3.refs_1_), custom_call_target="tpu_custom_call", output_to_operand_aliasing={{}: (1, {})} | custom-call | flops 4718592 | bytes 37748736 | tf_op jit(solution)/shard_map/place/pallas_call | solution.py:715
  528.3 0.0 copy-start.1
  528.3 35.5 %all-gather.4.cloned.1.call-done.refs_0_ = f32[64,576,128]{2,1,0:T(8,128)} async-done(((f32[1,576,128]{2,1,0:T(8,128)}), f32[64,576,128]{2,1,0:T(8,128)}) %all-gather.4.cloned.1.call-update) | async-done | bytes 18874384 | tf_op jit(solution)/shard_map/all_gather | solution.py:761
  563.7 14.1 %place.5 = f32[576,24576]{1,0:T(8,128)} custom-call(f32[64,576,128]{2,1,0:T(8,128)} %all-gather.4.cloned.1.call-done.refs_0_, f32[576,24576]{1,0:T(8,128)} %place.4.refs_1_), custom_call_target="tpu_custom_call", output_to_operand_aliasing={{}: (1, {})} | custom-call | flops 4718592 | bytes 37748736 | tf_op jit(solution)/shard_map/place/pallas_call | solution.py:715
  577.8 0.0 copy-done.1
  577.8 1.0 copy.14
Async XLA Ops:
  7.2 493.0 %all-gather.8.cloned.1.call-start = ((), (), s32[]{:S(2)}) async-start(), calls=%async_computation.2 | async-start | bytes 19169280 | tf_op jit(solution)/shard_map/all_gather | solution.py:761
  182.4 331.8 %all-gather.6.cloned.1.call-start = ((), (), s32[]{:S(2)}) async-start(), calls=%async_computation.1 | async-start | bytes 19169280 | tf_op jit(solution)/shard_map/all_gather | solution.py:761
  341.8 222.0 %all-gather.4.cloned.1.call-start = ((), (), s32[]{:S(2)}) async-start(), calls=%async_computation | async-start | bytes 19169280 | tf_op jit(solution)/shard_map/all_gather | solution.py:761
  472.2 4.5 collective-permute-start
  476.7 1.5 copy-start
  528.3 49.5 %copy-start.1 = (bf16[576,1024]{1,0:T(8,128)(2,1)S(1)}, bf16[576,1024]{1,0:T(8,128)(2,1)}, u32[]{:S(2)}) copy-start(bf16[576,1024]{1,0:T(8,128)(2,1)} %get-tuple-element.25) | copy-start | bytes 3538948
Sparse Core Ops, SparseCore 0:
  182.5 156.9 all-gather.7
  342.3 108.2 all-gather.5
  453.4 110.2 all-gather.3

commit v3 on v0

v3 whole, which is shorter than its diff:
```python
import jax
import jax.numpy as jnp
from jax import lax
from jax.experimental import pallas as pl
from jax.experimental.pallas import tpu as pltpu
from jax.sharding import Mesh, PartitionSpec as P

SOFT_CAP = 30.0
INV_CAP = 1.0 / SOFT_CAP
CAP_LOG2E = SOFT_CAP * 1.4426950408889634
LANES = 128
SUB = 8
RING = 4
WAYS = (1, RING - 1)
PAIR = range(2)
VMEM_LIMIT = 60 * 1024 * 1024
F32 = jnp.float32
BF16 = jnp.bfloat16
FAR = -(2 ** 22)
MESH_ID = pl.DeviceIdType.MESH
AXES = ('z', 'y', 'x', 'core')
CUBE = ('x', 'y', 'z')
SIZES = {'z': RING, 'y': RING, 'x': RING, 'core': 2}
SEM = pltpu.SemaphoreType.DMA
HBM = pl.BlockSpec(memory_space=pl.ANY)
SMEM = pl.BlockSpec(memory_space=pltpu.SMEM)
VMEM = pl.BlockSpec(memory_space=pltpu.VMEM)


def dot_f32(a, b, dims):
    return lax.dot_general(a, b, (dims, ((), ())), preferred_element_type=F32)


def f32(*shape):
    return jax.ShapeDtypeStruct(shape, F32)


def bf16(*shape):
    return jax.ShapeDtypeStruct(shape, BF16)


def block(axis, *shape):
    return pl.BlockSpec(shape, lambda i: tuple(i if n == axis else 0 for n in range(len(shape))))


def cost(flops, moved, exps=0):
    return pl.CostEstimate(flops=flops, bytes_accessed=moved, transcendentals=exps)


def params(**kw):
    return pltpu.CompilerParams(vmem_limit_bytes=VMEM_LIMIT, **kw)


def meeting(ident):
    return params(collective_id=ident, has_side_effects=True)


def lane_slice(j):
    return slice(j * LANES, (j + 1) * LANES)


def halved(n):
    return n // (2 * SUB) * SUB


def peer(**shift):
    place = []
    for axis in AXES:
        here = lax.axis_index(axis)
        if axis in shift:
            here = lax.rem(here + shift[axis], SIZES[axis])
        place.append(here)
    return tuple(place)


def send(src, dst, send_sem, recv_sem, where):
    return pltpu.make_async_remote_copy(
        src, dst, send_sem, recv_sem, device_id=where, device_id_type=MESH_ID)


def start(copies):
    for copy in copies:
        copy.start()


def finish(copies):
    for copy in copies:
        copy.wait()


def arrive(copies):
    for copy in copies:
        copy.wait_recv()


def meet(peers):
    barrier = pltpu.get_barrier_semaphore()
    for where in peers:
        pl.semaphore_signal(barrier, inc=1, device_id=where, device_id_type=MESH_ID)
    pl.semaphore_wait(barrier, len(peers))


def others(axis):
    return [peer(**{axis: r}) for r in range(1, SIZES[axis])]


def swap_copies(k, cur_ref, slot_ref, sends, recvs):
    axis = CUBE[k]
    return [send(cur_ref.at[k], slot_ref.at[k, lax.axis_index(axis)], sends.at[k, n],
                 recvs.at[k, n], where) for n, where in enumerate(others(axis))]


def swap_sum(k, cur_ref, slot_ref, sends, recvs):
    finish(swap_copies(k, cur_ref, slot_ref, sends, recvs))
    axis = CUBE[k]
    slot_ref[k, lax.axis_index(axis)] = cur_ref[k]
    total = slot_ref[k, 0]
    for i in range(1, SIZES[axis]):
        total = total + slot_ref[k, i]
    cur_ref[k + 1] = total


def swap_scratch(width):
    n = len(CUBE)
    return [pltpu.VMEM((n + 1, SUB, width), F32), pltpu.VMEM((n, RING, SUB, width), F32),
            SEM((n, n)), SEM((n, n))]


def norm_body(ht_ref, w1_ref, xt_ref, xb_ref):
    h = ht_ref[...].astype(F32)
    inv_rms = lax.rsqrt(jnp.mean(h * h, axis=0, keepdims=True) + 1e-6)
    xt = h * inv_rms * jnp.broadcast_to(w1_ref[:, :1], h.shape)
    xt_ref[0] = xt
    xb_ref[...] = xt.T.astype(BF16)


def norm_rows(ht, w1):
    dim, tokens = ht.shape
    tb = tokens // 2
    return pl.pallas_call(
        norm_body,
        grid=(2,),
        in_specs=[block(1, dim, tb), block(None, dim, LANES)],
        out_specs=[block(0, 1, dim, tb), block(0, tb, dim)],
        out_shape=[f32(2, dim, tb), bf16(tokens, dim)],
        compiler_params=params(),
        cost_estimate=cost(10 * ht.size, 8 * ht.size),
        name="norm",
    )(ht, w1)


def norm_back_body(ht_ref, w1_ref, g0_ref, g1_ref, loss_ref, dh_ref, sum_ref, dw_ref, *swap):
    step = pl.program_id(0)
    dim, tb = ht_ref.shape
    h = ht_ref[...].astype(F32)
    inv_rms = lax.rsqrt(jnp.mean(h * h, axis=0, keepdims=True) + 1e-6)
    n = h * inv_rms
    g = g0_ref[...] + g1_ref[...]
    gn = g * n

    @pl.when(step == 0)
    def _():
        dw_ref[...] = jnp.zeros_like(dw_ref)

    part = dw_ref[...]
    for j in range(tb // LANES):
        part = part + gn[:, lane_slice(j)]
    dw_ref[...] = part
    w1 = jnp.broadcast_to(w1_ref[:, :1], h.shape)
    inner = jnp.mean(gn * w1, axis=0, keepdims=True)
    dh_ref[...] = ((g * w1 - n * inner) * inv_rms).astype(BF16)

    @pl.when(step == pl.num_programs(0) - 1)
    def _():
        cur_ref = swap[0]
        cur_ref[0] = jnp.zeros_like(cur_ref[0])
        cur_ref[0, 0:1, 0:dim] = jnp.sum(dw_ref[...].T, axis=0, keepdims=True)
        cur_ref[0, 1:2, 0:LANES] = loss_ref[0:1, :]
        meet([where for axis in CUBE for where in others(axis)])
        for k in range(len(CUBE)):
            start(swap_copies(k, *swap))
            swap_sum(k, *swap)
        sum_ref[...] = cur_ref[len(CUBE)]


def norm_back(ht, w1, g0, g1, loss_tile):
    dim, tokens = ht.shape
    tb = tokens // 2
    width = -(-dim // LANES) * LANES
    cols = block(1, dim, tb)
    return pl.pallas_call(
        norm_back_body,
        grid=(2,),
        in_specs=[cols, block(None, dim, LANES), cols, cols, block(None, SUB, LANES)],
        out_specs=[cols, block(None, SUB, width)],
        out_shape=[bf16(dim, tokens), f32(SUB, width)],
        scratch_shapes=[pltpu.VMEM((dim, LANES), F32), *swap_scratch(width)],
        compiler_params=meeting(3),
        cost_estimate=cost(20 * ht.size, 12 * ht.size),
        name="norm_back",
    )(ht, w1, g0, g1, loss_tile)


GAP = 4


def fwd_body(tb, early, late, x_ref, lab_ref, mask_ref, row_ref, e_ref, xt_ref,
             xg_ref, stat_ref, count_ref, z_ref, p_ref, pay_ref, ring_sem, half_sem, die_sem,
             stat_sem, own_sem, *swap):
    step = pl.program_id(0)
    tokens = x_ref.shape[0]
    dim, bv = e_ref.shape
    cut = halved(dim)
    spans = (pl.ds(0, cut), pl.ds(cut, dim - cut))
    core = lax.axis_index('core')
    across = peer(core=1)
    group = [peer(x=r, core=c) for r in range(1, RING) for c in PAIR]
    ring = [send(xt_ref.at[core], xg_ref.at[2 * w, core], ring_sem.at[0, w], ring_sem.at[1, w],
                 peer(x=WAYS[w])) for w in PAIR]
    on = [send(xg_ref.at[2 * w, core, spans[w]], xg_ref.at[1, core, spans[w]],
               half_sem.at[0, w], half_sem.at[1, w], peer(x=WAYS[w])) for w in PAIR]
    over = [send(xg_ref.at[r, core], xg_ref.at[r, core], die_sem.at[0, r], die_sem.at[1, r],
                 across) for r in range(RING - 1)]

    @pl.when(step == 0)
    def _():
        z_ref[...] = jnp.zeros_like(z_ref)
        p_ref[...] = jnp.zeros_like(p_ref)
        cur_ref = swap[0]
        cur_ref[0] = jnp.full(cur_ref.shape[1:], jnp.sum(mask_ref[...]), F32)
        meet(others('y') + others('z') + group + [across])

    for k in range(len(CUBE) + 1):
        @pl.when(step == k * GAP)
        def _(k=k):
            if k:
                swap_sum(k - 1, *swap)
            if k < len(CUBE):
                start(swap_copies(k, *swap))
            else:
                count_ref[...] = swap[0][k]
            if not k:
                start(ring)

    @pl.when(step == early)
    def _():
        finish(ring)
        start(on)
        start(over[::2])

    @pl.when(step == late)
    def _():
        finish(on)
        over[1].start()

    lane = lax.broadcasted_iota(jnp.int32, (tb, LANES), 1)

    def rows_part(i, carry):
        rows = pl.ds(pl.multiple_of(i * tb, tb), tb)
        z = dot_f32(x_ref[rows, :], e_ref[...], ((1,), (0,)))
        lab = lab_ref[rows, :] - step * bv
        zsum = z_ref[rows, :]
        psum = p_ref[rows, :]
        for j in range(bv // LANES):
            t = jnp.tanh(z[:, lane_slice(j)] * INV_CAP)
            zsum = zsum + jnp.exp2(t * CAP_LOG2E)
            psum = jnp.where(lab == lane + j * LANES, t, psum)
        z_ref[rows, :] = zsum
        p_ref[rows, :] = psum
        return carry

    lax.fori_loop(0, tokens // tb, rows_part, 0, unroll=True)

    @pl.when(step == pl.num_programs(0) - 1)
    def _():
        pay_ref[...] = jnp.concatenate(
            [jnp.sum(z_ref[...].T, axis=0, keepdims=True),
             jnp.sum(p_ref[...].T, axis=0, keepdims=True), row_ref[...]], axis=0)
        own = pltpu.make_async_copy(pay_ref, stat_ref.at[0, core], own_sem)
        own.start()
        copies = [send(pay_ref, stat_ref.at[(n + 1) // 2, core], stat_sem.at[0, n],
                       stat_sem.at[1, n], where) for n, where in enumerate([across] + group)]
        start(copies)
        finish(over)
        own.wait()
        finish(copies)


def forward(x, lab_rep, mask_tile, lab_row, et, xt, bv=512, tb=256):
    tokens, dim = x.shape
    vocab = et.shape[1]
    tb = min(tb, tokens)
    steps = vocab // bv
    after = len(CUBE) * GAP + 1
    early, late = max(after, steps * 9 // 16), max(after + 1, steps * 5 // 6)
    per_lane = pltpu.VMEM((tokens, LANES), F32)
    return pl.pallas_call(
        lambda *refs: fwd_body(tb, early, late, *refs),
        grid=(steps,),
        in_specs=[block(None, tokens, dim), block(None, tokens, LANES),
                  block(None, SUB, tokens // SUB), block(None, 1, tokens), block(1, dim, bv), HBM],
        out_specs=[HBM, HBM, block(None, SUB, LANES)],
        out_shape=[f32(RING - 1, 2, dim, tokens // 2), f32(RING, 2, 3, tokens), f32(SUB, LANES)],
        scratch_shapes=[
            per_lane, per_lane, pltpu.VMEM((3, tokens), F32),
            SEM((2, 2)), SEM((2, 2)), SEM((2, RING)), SEM((2, SUB)), SEM, *swap_scratch(LANES)],
        compiler_params=meeting(1),
        cost_estimate=cost(2 * x.size * vocab, 2 * et.size, 2 * tokens * vocab),
        name="fwd",
    )(x, lab_rep, mask_tile, lab_row, et, xt)


def prep_body(cnt_ref, own_ref, xg_ref, stat_ref, xb_ref, xt_ref, scale_ref, lab_ref, loss_ref):
    r = pl.program_id(0)
    _, dim, half = own_ref.shape
    inv_count = cnt_ref[0]
    whole, tail = divmod(dim, LANES)

    def store(x_ref):
        for side in PAIR:
            v = x_ref[side]
            vt = v.T.astype(BF16)
            vb = v.astype(BF16)
            rows = pl.ds(side * half, half)
            for k in range(whole):
                xb_ref[k, rows, :] = vt[:, lane_slice(k)]
            if tail:
                xb_ref[whole, rows, :] = jnp.concatenate(
                    [vt[:, dim - tail:], jnp.zeros((half, LANES - tail), BF16)], axis=1)
            for k in range(half // LANES):
                xt_ref[side * (half // LANES) + k] = vb[:, lane_slice(k)]

    @pl.when(r == 0)
    def _():
        store(own_ref)

    @pl.when(r != 0)
    def _():
        store(xg_ref.at[0])

    def stat(n):
        return stat_ref[0, 0, pl.ds(n, 1), :], stat_ref[0, 1, pl.ds(n, 1), :]

    row_sum = sum(stat(0))
    label = stat(2)[0]
    live = label >= 0.0
    scale = jnp.where(live, inv_count, 0.0) / row_sum
    for k in range(2 * half // LANES):
        cols = lane_slice(k)
        scale_ref[cols, :] = jnp.broadcast_to(scale[:, cols], (LANES, LANES)).T
        lab_ref[cols, :] = jnp.broadcast_to(label[:, cols], (LANES, LANES)).T.astype(jnp.int32)

    @pl.when(r == 0)
    def _():
        picked = sum(stat(1)) * SOFT_CAP
        loss = jnp.where(live, jnp.log(row_sum) - picked, 0.0)
        loss_ref[...] = jnp.full(loss_ref.shape, jnp.sum(loss), F32)


def prep(inv_count, xt_own, xg, stat):
    _, dim, half = xt_own.shape
    tokens = 2 * half
    slabs = -(-dim // LANES)
    per = tokens // LANES
    group = RING * tokens
    return pl.pallas_call(
        prep_body,
        grid=(RING,),
        in_specs=[
            SMEM,
            block(None, 2, dim, half),
            pl.BlockSpec((1, 2, dim, half), lambda i: (jnp.maximum(i - 1, 0), 0, 0, 0)),
            block(0, 1, *stat.shape[1:]),
        ],
        out_specs=[
            block(1, slabs, tokens, LANES),
            block(0, per, dim, LANES),
            block(0, tokens, LANES),
            block(0, tokens, LANES),
            block(None, SUB, LANES),
        ],
        out_shape=[
            bf16(slabs, group, LANES), bf16(group // LANES, dim, LANES), f32(group, LANES),
            jax.ShapeDtypeStruct((group, LANES), jnp.int32), f32(SUB, LANES),
        ],
        compiler_params=params(),
        cost_estimate=cost(40 * xg.size, 8 * xg.size),
        name="prep",
    )(inv_count, xt_own, xg, stat)


def grad_tile(z, scale, lab, vid, inv_count):
    t = jnp.tanh(z * INV_CAP)
    p = jnp.exp2(t * CAP_LOG2E) * scale
    p = jnp.where(lab == vid, p - inv_count, p)
    return (p * (1.0 - t * t)).astype(BF16)


GATHERS = ('xyz', 'yzx', 'zxy')
STEPS = (' a', 'a A', 'A bc', 'b Bdf', 'Bc eC', 'df DF', 'e E', 'CDFE ')
LETTERS = 'abcdef'
WHEN = (10, 11, 12, 15, 18, 20, 22, 25)


def main_body(n_chunks, tb, rb, cnt_ref, off_ref, xb_ref, xt_ref, scale_ref, lab_ref, et_ref,
              ag_ref, gx_ref, ebuf, rbuf, ga_ref, gb_ref, gr_ref, shard, tiles, part_in, tile_in,
              bpart_in, btile_in, esem, fsem, own_sem, psend, precv, tsend, trecv,
              bpsend, bprecv, btsend, btrecv, agsend, agrecv):
    slabs, group_tokens, _ = xb_ref.shape
    dim, tokens = gx_ref.shape
    deep = slabs * LANES
    wide = rbuf.shape[1]
    blocks = group_tokens // tb
    cut = halved(dim)
    rest = dim - cut
    units = 8 * n_chunks
    row_units = et_ref.shape[1] // (wide * LANES)
    inv_count = cnt_ref[0]
    vocab_off = off_ref[0]
    me = {axis: lax.axis_index(axis) for axis in AXES}
    lane = lax.broadcasted_iota(jnp.int32, (tb, LANES), 1)
    side = 7 * dim // 24 // SUB * SUB
    ranges = ((0, side), (side, dim - 2 * side), (dim - side, side))

    def shifted(q, da, db):
        odd = lax.rem(q // 4, 2)
        return peer(z=db + odd * (da - db), y=da + odd * (db - da))

    def tile_index(u, j):
        k = u // 8
        odd = lax.rem(k, 2)
        s = lax.rem(u, 8) // 2
        half = lax.rem(u, 2)
        db = lax.rem(2 + 3 * s + 3 * (s * (s - 1) // 2), RING)
        da = 2 + half - j * (1 + 2 * half)
        dz, dy = db + odd * (da - db), da + odd * (db - da)
        return ((k * RING + lax.rem(me['z'] + dz, RING)) * RING
                + lax.rem(me['y'] + dy, RING)) * SIZES['x'] + me['x']

    def fetch(u, j):
        cols = pl.ds(pl.multiple_of(tile_index(u, j) * LANES, LANES), LANES)
        slot = lax.rem(u, 2)
        return pltpu.make_async_copy(
            et_ref.at[:, cols], ebuf.at[slot, j, pl.ds(0, dim)], esem.at[slot, j])

    def fetch_wide(v, j):
        cols = pl.ds(pl.multiple_of((v * wide + j) * LANES, LANES), LANES)
        slot = lax.rem(v, 2)
        return pltpu.make_async_copy(
            et_ref.at[:, cols], rbuf.at[slot, j, pl.ds(0, dim)], fsem.at[slot, j])

    def parts(src, dst, sends, recvs, q, da, db):
        return (send(src.at[pl.ds(0, cut)], dst.at[0, pl.ds(0, cut)], sends.at[0], recvs.at[0],
                     shifted(q, da, db)),
                send(src.at[pl.ds(cut, rest)], dst.at[1, pl.ds(0, rest)], sends.at[1],
                     recvs.at[1], shifted(q, 3 * da, 3 * db)))

    def part_copies(q):
        return parts(tiles.at[q, 0], part_in.at[q], psend.at[q], precv.at[q], q, 1, 0)

    def bpart_copies(k):
        return parts(tiles.at[4 * k, 3], bpart_in.at[k], bpsend.at[k], bprecv.at[k], 4 * k, 0, 1)

    def tile_copies(q):
        return [send(tiles.at[q, 1 + w], tile_in.at[q, w], tsend.at[q, w], trecv.at[q, w],
                     shifted(q, WAYS[w], 0)) for w in PAIR]

    def btile_copies(k):
        return [send(tiles.at[4 * k + 1 + w, 3], btile_in.at[k, w], btsend.at[k, w],
                     btrecv.at[k, w], shifted(4 * k, 0, WAYS[w])) for w in PAIR]

    def add_parts(first, second, got):
        first[0:cut, :] += got[0, 0:cut, :]
        second[cut:dim, :] += got[1, 0:rest, :]

    def close_slab(q):
        arrive(tile_copies(q))
        tiles[q, 3] = tiles[q, 3] + (tile_in[q, 0] + tile_in[q, 1])

    def close_chunk(k):
        close_slab(4 * k + 3)
        arrive(btile_copies(k))
        shard[k] = tiles[4 * k + 3, 3] + (btile_in[k, 0] + btile_in[k, 1])

    def own_copy(k):
        return pltpu.make_async_copy(
            shard.at[k], ag_ref.at[k, me['z'], me['y'], me['x']], own_sem.at[k])

    def hops(k, letter):
        block = LETTERS.index(letter.lower())
        passed = int(letter.isupper())
        out = []
        for p, order in enumerate(GATHERS):
            phase = min(block, 2)
            axis = order[phase]
            if SIZES[axis] == 1 or (phase == 2 and block - 2 >= SIZES[order[1]]):
                continue
            for w in PAIR:
                at = dict(me)
                for done in order[:phase]:
                    at[done] = pl.ds(0, SIZES[done])
                if phase == 2:
                    at[order[1]] = lax.rem(me[order[1]] + block - 2, SIZES[order[1]])
                low, high = ranges[p]
                if passed:
                    at[axis] = lax.rem(me[axis] + RING - WAYS[w], RING)
                    mid = halved(high)
                    low, high = (low + mid, high - mid) if w else (low, mid)
                there = ag_ref.at[k, at['z'], at['y'], at['x'], pl.ds(low, high)]
                here = there if block + passed else shard.at[k, pl.ds(low, high)]
                sems = (k, p, block, passed, w)
                out.append(send(here, there, agsend.at[sems], agrecv.at[sems],
                                peer(**{axis: WAYS[w]})))
        return out

    def gather_step(k, n):
        waits, starts = STEPS[n].split(' ')
        for letter in waits:
            arrive(hops(k, letter))
        if n == 0:
            own_copy(k).start()
        if n == 2:
            own_copy(k).wait()
        for letter in starts:
            start(hops(k, letter))

    def gather_ticks(u, low, high):
        for n, due in enumerate(WHEN):
            if due < high and due + units > low:
                k = (u - due) // 8

                @pl.when((u >= due) & (k < n_chunks) & (lax.rem(u - due + 8, 8) == 0))
                def _(k=k, n=n):
                    gather_step(k, n)

    if deep > dim:
        zeros = jnp.zeros((deep - dim, LANES), BF16)
        for slot in PAIR:
            for j in PAIR:
                ebuf[slot, j, dim:, :] = zeros
            for j in range(wide):
                rbuf[slot, j, dim:, :] = zeros
    start([fetch(0, j) for j in PAIR])
    meet([peer(**{axis: w}) for axis in CUBE if SIZES[axis] > 1 for w in WAYS])

    def table_unit(u, carry):
        slot = lax.rem(u, 2)
        q = u // 2
        k = u // 8
        s = lax.rem(q, 4)
        half = slot
        for j in PAIR:
            fetch(u, j).wait()

        @pl.when(u + 1 < units)
        def _():
            start([fetch(u + 1, j) for j in PAIR])

        bases = [tile_index(u, j) * LANES + vocab_off for j in PAIR]

        def grads(i, g_ref):
            rows = pl.ds(pl.multiple_of(i * tb, tb), tb)
            x = jnp.concatenate([xb_ref[n, rows, :] for n in range(slabs)], axis=1)
            e = jnp.concatenate([ebuf[slot, 0], ebuf[slot, 1]], axis=1)
            z = dot_f32(x, e, ((1,), (0,)))
            lab = lab_ref[rows, :]
            scale = scale_ref[rows, :]
            for j in PAIR:
                g_ref[j] = grad_tile(z[:, lane_slice(j)], scale, lab - bases[j], lane,
                                     inv_count)

        def product(i, g_ref, store):
            n = tb // LANES
            x = jnp.concatenate([xt_ref[i * n + m] for m in range(n)], axis=1)
            g = jnp.concatenate([g_ref[0], g_ref[1]], axis=1)
            part = dot_f32(x, g, ((1,), (0,)))
            for j in PAIR:
                store(2 * half + j, part[:, lane_slice(j)])

        def put(t, part):
            tiles[q, t] = part

        def add(t, part):
            tiles[q, t] += part

        grads(0, ga_ref)
        grads(1, gb_ref)
        product(0, ga_ref, put)

        def both(i, c):
            grads(2 * i, ga_ref)
            product(2 * i - 1, gb_ref, add)
            grads(2 * i + 1, gb_ref)
            product(2 * i, ga_ref, add)
            return c

        lax.fori_loop(1, blocks // 2, both, 0)
        product(blocks - 1, gb_ref, add)

        @pl.when(half == 0)
        def _():
            @pl.when((s == 1) & (k > 0))
            def _():
                close_chunk(k - 1)

            start(part_copies(q))

        @pl.when(half == 1)
        def _():
            arrive(part_copies(q))
            add_parts(tiles.at[q, 1], tiles.at[q, 2], part_in.at[q])

            @pl.when(s >= 1)
            def _():
                close_slab(q - 1)

            start(tile_copies(q))

            @pl.when(s == 1)
            def _():
                start(bpart_copies(k))

            @pl.when(s == 3)
            def _():
                arrive(bpart_copies(k))
                add_parts(tiles.at[4 * k + 1, 3], tiles.at[4 * k + 2, 3], bpart_in.at[k])
                start(btile_copies(k))

        gather_ticks(u, 0, units)
        return carry

    lax.fori_loop(0, units, table_unit, 0)

    row_lane = lax.broadcasted_iota(jnp.int32, (rb, LANES), 1)
    start([fetch_wide(0, j) for j in range(wide)])
    gx_ref[...] = jnp.zeros_like(gx_ref)

    def row_unit(v, carry):
        slot = lax.rem(v, 2)
        for j in range(wide):
            fetch_wide(v, j).wait()

        @pl.when(v + 1 < row_units)
        def _():
            start([fetch_wide(v + 1, j) for j in range(wide)])

        base = v * wide * LANES + vocab_off

        def block(i, c):
            rows = pl.ds(pl.multiple_of(i * rb, rb), rb)
            x = jnp.concatenate([xb_ref[n, rows, :] for n in range(slabs)], axis=1)
            e = jnp.concatenate([rbuf[slot, j] for j in range(wide)], axis=1)
            z = dot_f32(x, e, ((1,), (0,)))
            lab = lab_ref[rows, :] - base
            scale = scale_ref[rows, :]
            for j in range(wide):
                gr_ref[:, lane_slice(j)] = grad_tile(
                    z[:, lane_slice(j)], scale, lab, row_lane + j * LANES, inv_count)
            e = jnp.concatenate([rbuf[slot, j, 0:dim, :] for j in range(wide)], axis=1)
            gx_ref[:, rows] += dot_f32(e, gr_ref[...], ((1,), (1,)))
            return c

        lax.fori_loop(0, tokens // rb, block, 0)

        @pl.when(v == 2)
        def _():
            close_chunk(n_chunks - 1)

        gather_ticks(v + units, units, units + row_units)
        return carry

    lax.fori_loop(0, row_units, row_unit, 0)

    def sent(q, carry):
        for copy in (*part_copies(q), *tile_copies(q)):
            copy.wait_send()
        return carry

    lax.fori_loop(0, 4 * n_chunks, sent, 0)

    def sent_chunk(k, carry):
        for copy in (*bpart_copies(k), *btile_copies(k)):
            copy.wait_send()
        for letter in LETTERS + LETTERS.upper():
            for copy in hops(k, letter):
                copy.wait_send()
        return carry

    lax.fori_loop(0, n_chunks, sent_chunk, 0)


def backward(inv_count, vocab_off, xb, xt, scale, lab, et, tb=512, rb=256, wide=8):
    slabs, group_tokens, _ = xb.shape
    dim = xt.shape[1]
    vocab = et.shape[1]
    tokens = group_tokens // SIZES['x']
    cube = tuple(SIZES[axis] for axis in AXES[:3])
    n_chunks = vocab // (LANES * cube[0] * cube[1] * cube[2])
    tb, rb = min(tb, group_tokens // 4), min(rb, tokens)
    part = dim - halved(dim)
    q = RING * n_chunks
    tile = (dim, LANES)
    held = (slabs * LANES, LANES)

    def vmem(dtype, *shape):
        return pltpu.VMEM(shape, dtype)

    return pl.pallas_call(
        lambda *refs: main_body(n_chunks, tb, rb, *refs),
        in_specs=[SMEM, SMEM, VMEM, VMEM, VMEM, VMEM, HBM],
        out_specs=[HBM, VMEM],
        out_shape=[f32(n_chunks, *cube, *tile), f32(dim, tokens)],
        scratch_shapes=[
            vmem(BF16, 2, 2, *held), vmem(BF16, 2, wide, *held),
            vmem(BF16, 2, tb, LANES), vmem(BF16, 2, tb, LANES), vmem(BF16, rb, wide * LANES),
            vmem(F32, n_chunks, *tile), vmem(F32, q, RING, *tile),
            vmem(F32, q, 2, part, LANES), vmem(F32, q, 2, *tile),
            vmem(F32, n_chunks, 2, part, LANES), vmem(F32, n_chunks, 2, *tile),
            SEM((2, 2)), SEM((2, wide)), SEM((n_chunks,)),
            *[SEM((q, 2))] * 4,
            *[SEM((n_chunks, 2))] * 4,
            *[SEM((n_chunks, len(GATHERS), len(LETTERS), 2, 2))] * 2,
        ],
        compiler_params=meeting(2),
        cost_estimate=cost(8 * xt.size * vocab, 4 * et.size),
        name="backward",
    )(inv_count, vocab_off, xb, xt, scale, lab, et)


def place_body(n, src_ref, out_ref):
    for k in range(n):
        out_ref[:, lane_slice(k)] = src_ref[0, k]


def place(gathered):
    n_chunks, n_dev, dim, _ = gathered.shape
    rows = dim // 6 if dim % 48 == 0 else dim
    return pl.pallas_call(
        lambda *refs: place_body(n_dev, *refs),
        grid=(n_chunks, dim // rows),
        in_specs=[pl.BlockSpec((1, n_dev, rows, LANES), lambda c, i: (c, 0, i, 0))],
        out_specs=pl.BlockSpec((rows, n_dev * LANES), lambda c, i: (i, c)),
        out_shape=f32(dim, n_chunks * n_dev * LANES),
        compiler_params=params(),
        cost_estimate=cost(gathered.size, 8 * gathered.size),
        name="place",
    )(gathered)


def solution(mesh):
    grid_mesh = Mesh(mesh.devices.reshape(RING, RING, RING, 2), AXES)
    dp = AXES[:3]

    def local_step(hidden, norm_w, embed_table, labels, loss_mask):
        batch_rows, seq_len, dim = hidden.shape
        vocab = embed_table.shape[0]
        tokens = batch_rows * seq_len
        et = embed_table.T
        ht = hidden.reshape(tokens, dim).T
        w1 = jnp.broadcast_to((1.0 + norm_w.astype(F32))[:, None], (dim, LANES))
        mask_row = loss_mask.reshape(1, tokens)
        lab_row = labels.reshape(1, tokens)
        core = lax.axis_index('core')

        xt_own, xb_own = norm_rows(ht, w1)
        lab_rep = jnp.broadcast_to((lab_row.reshape(tokens) - core * vocab)[:, None], (tokens, LANES))
        lab_live = jnp.where(mask_row > 0, lab_row, FAR).astype(F32)
        xg, stat, count = forward(
            xb_own, lab_rep, mask_row.reshape(SUB, tokens // SUB).astype(F32), lab_live, et, xt_own)
        inv_count = (1.0 / jnp.maximum(count[0, 0], 1.0)).reshape(1)
        vocab_off = (core * vocab).astype(jnp.int32).reshape(1)
        xb, xt, scale, lab, loss_tile = prep(inv_count, xt_own, xg, stat)

        gathered, gxt = backward(inv_count, vocab_off, xb, xt, scale, lab, et)
        table = place(gathered.reshape(-1, RING ** 3, dim, LANES))
        dht, sums = norm_back(
            ht, w1, gxt, lax.ppermute(gxt, 'core', [(0, 1), (1, 0)]), loss_tile)
        return (sums[1, 0] * inv_count[0], dht.T.reshape(batch_rows, seq_len, dim),
                sums[0, :dim], table.T)

    return jax.shard_map(
        local_step, mesh=grid_mesh,
        in_specs=(P(dp, None, None), P(None), P('core', None), P(dp, None), P(dp, None)),
        out_specs=(P(), P(dp, None, None), P(None), P('core', None)), check_vma=False)
```

time: 975 us -> 545 us (0.56)
  Pallas kernels: 0 us -> 530 us
  blocking collectives: 366 us -> 0 us
  waiting for transfers between devices: 296 us -> 0.01 us
  matrix products: 141 us -> 0 us
  other arithmetic: 116 us -> 2.06 us
  local copies, waits for them, and re-layouts: 39.8 us -> 9.34 us
  between operations: 16.6 us -> 3.15 us
    pallas_call x0 -> x6, Pallas kernels: none -> 530 us  [the longest x1 385 us: backward(): pl.pallas_call(lambda *refs: main_body(n_chunks, tb, rb, *refs), in_specs...]
    psum x3 -> x0, blocking collectives: 363 us -> none  [the longest x1 181 us: local_step(): tok_count = jnp.maximum(lax.psum(jnp.sum(mask_rows), 'dp'), 1.0)]
    psum x2 -> x0, waiting for transfers between devices: 296 us -> none  [the longest x1 296 us: local_step(): grad_table = lax.psum(table_part, 'dp')]
    dot_general x3 -> x0, matrix products: 141 us -> none  [the longest x1 57.4 us: local_step(): jnp.einsum('td,vd->tv', normed_bf, embed_table, preferred_element_type=jn...]
    convert_element_type x2 -> x1, other arithmetic: 59.2 us -> 1.37 us  [local_step(): lab_live = jnp.where(mask_row > 0, lab_row, FAR).astype(F32)]
    reduce_sum x4 -> x0, other arithmetic: 50.5 us -> none  [the longest x1 45.2 us: local_step(): row_sum = lax.psum(jnp.sum(exp_shift, axis=-1), 'tp')]
    unnamed x17 -> x3, local copies, waits for them, and re-layouts: 39.8 us -> 3.78 us
  transfers between devices with their start and end apart: 2 -> 1, of which waited for: 1 -> 0; matrix products, arithmetic and copies ran while one was open for 5% -> 0% of each run, Pallas kernels for 0% -> 8%
where the time goes in v3:
time: 545 us; the launch traced here: 544 us
  Pallas kernels  530 us (97%)
  local copies, waits for them, and re-layouts  9.34 us (2%)
    pallas_call x1, Pallas kernels, backward(): pl.pallas_call(lambda *refs: main_body(n_chunks, tb, rb, *refs), in_specs...  385 us
    pallas_call x1, Pallas kernels, forward(): pl.pallas_call(lambda *refs: fwd_body(tb, early, late, *refs), grid=(step...  69.3 us
    pallas_call x1, Pallas kernels, place(): pl.pallas_call(lambda *refs: place_body(n_dev, *refs), grid=(n_chunks, di...  41.6 us
    pallas_call x1, Pallas kernels, norm_back(): pl.pallas_call(norm_back_body, grid=(2,), in_specs=[cols, block(None, dim...  19.6 us
  transfers between devices with their start and end apart: 1, of which 0 were waited for; matrix products, arithmetic and copies ran while one was open for 0% of the time, Pallas kernels for 8%

profile of v3, /device:TPU:0, one launch (start us, length us, event | category | flops | bytes accessed | tf_op | source)
XLA Modules:
  0.0 544.3 jit_solution(15839048176697228694)
XLA Ops:
  0.6 0.7 convert_add_fusion
  1.3 0.9 broadcast_in_dim.7.w1_ref
  2.2 3.3 norm.1
  5.5 1.4 fusion
  6.9 1.0 broadcast_in_dim.8.refs_1_
  7.8 69.3 %fwd.1 = (f32[3,2,576,512]{3,2,1,0:T(8,128)}, f32[4,2,3,1024]{3,2,1,0:T(4,128)}, f32[8,128]{1,0:T(8,128)}) custom-call(bf16[1024,576]{1,0:T(8,128)(2,1)} %get-tuple-element.18.refs_0_, s32[1024,128]{1,0:T(8,128)} %broadcast_in_dim.8.refs_1_, f32[8,128]{1,0:T(8,128)} %bitcast.20, f32[1,1024]{1,0:T(1,128)} %get-tuple-element.32.refs_3_, ...), custom_call_target="tpu_custom_call" | custom-call | flops 28991029248 | bytes 28311552 | tf_op jit(solution)/shard_map/fwd/pallas_call | solution.py:297
  77.2 1.2 slice.9
  79.1 10.8 %prep.1 = (bf16[5,4096,128]{2,1,0:T(8,128)(2,1)}, bf16[32,576,128]{2,1,0:T(8,128)(2,1)}, f32[4096,128]{1,0:T(8,128)}, s32[4096,128]{1,0:T(8,128)}, f32[8,128]{1,0:T(8,128)}) custom-call(f32[1]{0:T(128)} %bitcast.6.cnt_ref.refs_0_, f32[2,576,512]{2,1,0:T(8,128)} %get-tuple-element.19.refs_5_.own_ref, f32[3,2,576,512]{3,2,1,0:T(8,128)} %get-tuple-element.21.xg_ref, ...), custom_call_target="tpu_custom_call" | custom-call | flops 70778880 | bytes 14155776 | tf_op jit(solution)/shard_map/prep/pallas_call | solution.py:366
  89.8 385.1 %backward.1 = (f32[3,4,4,4,576,128]{5,4,3,2,1,0:T(8,128)}, f32[576,1024]{1,0:T(8,128)}) custom-call(f32[1]{0:T(128)} %bitcast.6.cnt_ref.refs_0_, s32[1]{0:T(128)} %bitcast.7.refs_1_, bf16[5,4096,128]{2,1,0:T(8,128)(2,1)} %get-tuple-element.23.refs_2_, bf16[32,576,128]{2,1,0:T(8,128)(2,1)} %get-tuple-element.24.refs_3_, ...), custom_call_target="tpu_custom_call" | custom-call | flops 463856467968 | bytes 56623104 | tf_op jit(solution)/shard_map/backward/pallas_call | solution.py:708
  474.9 0.1 collective-permute-start
  475.0 41.6 %place.1 = f32[576,24576]{1,0:T(8,128)} custom-call(f32[3,64,576,128]{3,2,1,0:T(8,128)} %bitcast.15), custom_call_target="tpu_custom_call" | custom-call | flops 14155776 | bytes 113246208 | tf_op jit(solution)/shard_map/place/pallas_call | solution.py:738
  516.6 0.0 collective-permute-done.g1_ref
  516.6 0.0 copy-start
  516.6 1.4 copy-done
  518.0 19.6 %norm_back.1 = (bf16[576,1024]{1,0:T(8,128)(2,1)}, f32[8,640]{1,0:T(8,128)}) custom-call(bf16[576,1024]{1,0:T(8,128)(2,1)} %bitcast.17, f32[576,128]{1,0:T(8,128)} %broadcast_in_dim.7.w1_ref, f32[576,1024]{1,0:T(8,128)} %get-tuple-element.27.g0_ref, f32[576,1024]{1,0:T(8,128)} %copy-done, f32[8,128]{1,0:T(8,128)} %get-tuple-element.28.loss_ref), custom_call_target="tpu_custom_call" | custom-call | flops 11796480 | bytes 7077888 | tf_op jit(solution)/shard_map/norm_back/pallas_call | solution.py:191
  537.6 1.2 slice.10
  538.8 1.3 slice_reduce_fusion
  540.8 2.4 copy.10
Async XLA Ops:
  474.9 41.7 %collective-permute-start = (f32[576,1024]{1,0:T(8,128)}, f32[576,1024]{1,0:T(8,128)S(1)}, u32[]{:S(2)}, u32[]{:S(2)}) collective-permute-start(f32[576,1024]{1,0:T(8,128)} %get-tuple-element.27.g0_ref), channel_id=1, source_target_pairs={{0,1},{1,0},{2,3},{3,2},{4,5},{5,4},{6,7},{7,6},{8,9},{9,8},{10,11... | collective-permute-start | bytes 7077896 | tf_op jit(solution)/shard_map/ppermute | solution.py:777
  516.6 1.4 copy-start
